TPU v7x, 256 devices: a whole 4x4x8 slice. The times are simulated.
256 devices in a mesh: src: 8 (over y, x_lo), tx: 8 (over z), ty: 4 (over x_hi, core).
Axes of the slice: x: 4 (x_hi: 2, x_lo: 2; x = x_hi * 2 + x_lo), y: 4, z: 8, core: 2. Of those that a mesh axis runs over, the one named last changes fastest.
Arguments:
- spectra: bfloat16 [32, 3, 2, 256, 256], P('src'), may hold values from -2.5 to 2.5
- pupil_shift: int32 [32, 2], P('src'), may hold values from -121 to 121
- window_offset: int32 [32, 2], P('src'), may hold values from -3 to 3
- source_weight: float32 [32], replicated, may hold values from 0.3 to 3
- mask_codes: int32 [128, 128], replicated, may hold values from 0 to 3
- levels: float32 [2, 4], replicated, may hold values from -1 to 1
- quench_start: float32 [512, 16, 512], P(('src', 'tx'), None, 'ty'), may hold values from 0.4 to 1.2
Outputs:
- acid: float32 [512, 16, 512], P(('src', 'tx'), None, 'ty')
- quencher: float32 [512, 16, 512], P(('src', 'tx'), None, 'ty')
- inhibitor: float32 [512, 16, 512], P(('src', 'tx'), None, 'ty')
All inputs are finite; a program needn't handle non-finite values.
Results may differ from a plain program's by a relative error of at most 0.0014.
Values may be sent and summed in bfloat16 or wider, within the bound.
A program may use at most 128 MiB of HBM per device.

v0:
```python
import functools
import math

import jax
import jax.numpy as jnp
import numpy as np
from jax import lax
from jax.experimental import pallas as pl
from jax.experimental.pallas import tpu as pltpu
from jax.sharding import PartitionSpec as P

RADIUS = 124
CELL = 4
STEPS = 8
NX = 512
NY = 512
WIN = 256
DEPTH = 16
N_SRC, N_TX, N_TY = 8, 8, 4
ROWS, COLS = 8, 128
CELLS = 128

TWO_PI = 2.0 * math.pi
NUM_AP = 0.33
DZ_WAVE = 0.148
ABSORB = 0.05

HALF = math.pi * DZ_WAVE * (1.0 - math.sqrt(1.0 - NUM_AP * NUM_AP))
REACH = HALF * 7.5
TERMS = 5
PLANES = 8
MESH = pl.DeviceIdType.MESH


def fit(function, powers, reach):
    nodes = np.cos((2 * np.arange(400) + 1) * np.pi / 800)
    basis = np.stack([nodes**k for k in powers], 1)
    sides = np.linalg.lstsq(basis, function(reach * nodes), rcond=None)[0]
    return [float(v) for v in sides]


EVEN = fit(np.cos, (0, 2, 4), REACH)
ODD = fit(np.sin, (1, 3), REACH)
SCALE = [EVEN[0], ODD[0], -EVEN[1], -ODD[1], EVEN[2]]
PHASE_COS = fit(np.cos, (0, 2, 4, 6), 8.0 * HALF)
PHASE_SIN = fit(np.sin, (1, 3, 5), 8.0 * HALF)


def wave_tables():
    u = np.arange(WIN)
    left = np.zeros((N_TX, 2 * N_SRC * ROWS, 2 * WIN))
    for tx in range(N_TX):
        local = np.arange(N_SRC * ROWS)
        x = (local // ROWS * N_TX + tx) * ROWS + local % ROWS
        angle = TWO_PI / NX * ((x[:, None] * (u[None, :] - WIN // 2)) % NX)
        c, s = np.cos(angle), np.sin(angle)
        left[tx] = np.block([[c, -s], [s, c]])
    right = np.zeros((N_TY, 2 * WIN, 2 * COLS))
    for ty in range(N_TY):
        y = ty * COLS + np.arange(COLS)
        angle = TWO_PI / NY * ((y[None, :] * (u[:, None] - WIN // 2)) % NY)
        c, s = np.cos(angle), np.sin(angle)
        right[ty] = np.block([[c, s], [-s, c]])
    return left, right


def cell_tables():
    a = np.arange(CELLS)
    angle = TWO_PI / CELLS * ((a[:, None] * a[None, :]) % CELLS)
    c, s = np.cos(angle), np.sin(angle)
    by_column = np.block([[c, -s], [s, c]])
    by_row = np.block([[c, s], [-s, c]])
    orders = np.arange(NX) - NX // 2
    phase = TWO_PI / NX * ((orders[:, None] * np.arange(CELL)[None, :]) % NX)
    shape_re = np.cos(phase).sum(1) / NX
    shape_im = -np.sin(phase).sum(1) / NX
    shape = np.stack([shape_re, shape_im])
    shape_x = np.broadcast_to(shape[:, :, None], (2, NX, 128))
    shape_y = np.broadcast_to(shape[:, None, :], (2, 8, NY))
    return (
        by_column.astype(np.float32),
        by_row.astype(np.float32),
        shape_x.astype(np.float32),
        shape_y.astype(np.float32),
    )


def exact(left, right):
    return jnp.dot(
        left, right, precision=lax.Precision.HIGHEST, preferred_element_type=jnp.float32
    )


def image_kernel(
    shift_ref,
    offset_ref,
    levels_ref,
    weight_ref,
    all_weights_ref,
    codes_ref,
    by_column_ref,
    by_row_ref,
    shape_x_ref,
    shape_y_ref,
    spectra_ref,
    left_hbm,
    right_hbm,
    out_ref,
    left_ref,
    right_ref,
    cells_ref,
    operand_ref,
    half_ref,
    wave_ref,
    acc_ref,
    sems,
):
    j = pl.program_id(0)
    count = pl.num_programs(0)
    tables = (
        pltpu.make_async_copy(left_hbm.at[lax.axis_index("tx")], left_ref, sems.at[0]),
        pltpu.make_async_copy(right_hbm.at[lax.axis_index("ty")], right_ref, sems.at[1]),
    )

    @pl.when(j == 0)
    def _():
        for copy in tables:
            copy.start()
        codes = codes_ref[...]
        parts = []
        for part in range(2):
            grid = jnp.full(codes.shape, levels_ref[part, 3], jnp.float32)
            for level in range(3):
                grid = jnp.where(codes == level, levels_ref[part, level], grid)
            parts.append(grid)
        across = exact(jnp.concatenate(parts, axis=1), by_column_ref[...])
        both = jnp.concatenate([across[:, :CELLS], across[:, CELLS:]], axis=0)
        full = exact(by_row_ref[...], both)
        for part in range(2):
            piece = full[part * CELLS : (part + 1) * CELLS]
            cells_ref[part, 0:CELLS] = piece
            cells_ref[part, CELLS : 2 * CELLS] = piece
        acc_ref[...] = jnp.zeros_like(acc_ref)
        for copy in tables:
            copy.wait()

    first_x = offset_ref[j, 0] - shift_ref[j, 0] - WIN // 2
    first_y = offset_ref[j, 1] - shift_ref[j, 1] - WIN // 2
    start_x = first_x + NX // 2
    start_y = first_y + NY // 2
    cell_x = lax.rem(start_x, CELLS)
    roll_y = lax.rem(2 * CELLS - lax.rem(start_y, CELLS), CELLS)
    shape_y = [
        pltpu.roll(shape_y_ref[part], NY - start_y, 1)[:, :WIN] for part in range(2)
    ]
    y_re = jnp.concatenate([shape_y[0]] * 2, axis=0)
    y_im = jnp.concatenate([shape_y[1]] * 2, axis=0)
    freq_y = (
        lax.broadcasted_iota(jnp.int32, (16, WIN), 1) - WIN // 2 + offset_ref[j, 1]
    ).astype(jnp.float32)
    square_y = freq_y * freq_y
    row_in = lax.broadcasted_iota(jnp.int32, (16, WIN), 0) - WIN // 2 + offset_ref[j, 0]

    def build(step):
        at = pl.multiple_of(step * 16, 16)
        cell_at = lax.rem(cell_x + at, CELLS)
        g_re = pltpu.roll(cells_ref[0, pl.ds(cell_at, 16), :], roll_y, 1)
        g_im = pltpu.roll(cells_ref[1, pl.ds(cell_at, 16), :], roll_y, 1)
        x_re = shape_x_ref[0, pl.ds(start_x + at, 16), :]
        x_im = shape_x_ref[1, pl.ds(start_x + at, 16), :]
        gx_re = g_re * x_re - g_im * x_im
        gx_im = g_re * x_im + g_im * x_re
        gx_re = jnp.concatenate([gx_re, gx_re], axis=1)
        gx_im = jnp.concatenate([gx_im, gx_im], axis=1)
        thin_re = gx_re * y_re - gx_im * y_im
        thin_im = gx_re * y_im + gx_im * y_re
        freq_x = (row_in + at).astype(jnp.float32)
        radial = freq_x * freq_x + square_y
        limit = float(RADIUS * RADIUS)
        inside = radial <= limit
        axial = jnp.sqrt(1.0 - (NUM_AP / RADIUS) ** 2 * jnp.minimum(radial, limit))
        slope = TWO_PI * DZ_WAVE / HALF
        w = slope * (axial - 1.0) + 1.0
        square = w * w
        turn_re = jnp.full_like(w, PHASE_COS[-1])
        for value in PHASE_COS[-2::-1]:
            turn_re = turn_re * square + value
        turn_im = jnp.full_like(w, PHASE_SIN[-1])
        for value in PHASE_SIN[-2::-1]:
            turn_im = turn_im * square + value
        turn_im = turn_im * w
        zero = jnp.zeros_like(w)
        h_re = jnp.where(inside, thin_re * turn_re - thin_im * turn_im, zero)
        h_im = jnp.where(inside, thin_re * turn_im + thin_im * turn_re, zero)
        for c in range(3):
            f_re = spectra_ref[0, c, 0, pl.ds(at, 16), :].astype(jnp.float32)
            f_im = spectra_ref[0, c, 1, pl.ds(at, 16), :].astype(jnp.float32)
            s_re = f_re * h_re - f_im * h_im
            s_im = f_re * h_im + f_im * h_re
            for n in range(TERMS):
                where = slice((c * TERMS + n) * WIN, (c * TERMS + n + 1) * WIN)
                operand_ref[pl.ds(at, 16), where] = s_re.astype(jnp.bfloat16)
                operand_ref[pl.ds(WIN + at, 16), where] = s_im.astype(jnp.bfloat16)
                if n < TERMS - 1:
                    s_re = s_re * w
                    s_im = s_im * w

    @pl.loop(0, WIN // 16, unroll=2)
    def _(step):
        build(step)

    for block in range(3 * TERMS):
        halves = jnp.dot(
            left_ref[...],
            operand_ref[:, block * WIN : (block + 1) * WIN],
            preferred_element_type=jnp.float32,
        ).astype(jnp.bfloat16)
        half_ref[block * 64 : (block + 1) * 64, 0:WIN] = halves[0:64]
        half_ref[block * 64 : (block + 1) * 64, WIN : 2 * WIN] = halves[64:128]
    for c in range(3):
        span = slice(c * TERMS * 64, (c + 1) * TERMS * 64)
        wave_ref[span, :] = jnp.dot(
            half_ref[span, :], right_ref[...], preferred_element_type=jnp.float32
        )
    weight = weight_ref[lax.axis_index("src") * count + j]
    for p in range(N_SRC):
        totals = [None] * 9

        def gather(n, value):
            totals[n] = value if totals[n] is None else totals[n] + value

        for c in range(3):
            re, im = [], []
            for n in range(TERMS):
                base = (c * TERMS + n) * 64 + p * ROWS
                re.append(wave_ref[base : base + ROWS, 0:COLS] * SCALE[n])
                im.append(wave_ref[base : base + ROWS, COLS : 2 * COLS] * SCALE[n])

            def real(a, b):
                return re[a] * re[b] + im[a] * im[b]

            def imag(a, b):
                return im[a] * re[b] - re[a] * im[b]

            gather(0, real(0, 0))
            gather(1, -2.0 * imag(1, 0))
            gather(2, real(1, 1) - 2.0 * real(0, 2))
            gather(3, 2.0 * (imag(1, 2) + imag(3, 0)))
            gather(4, real(2, 2) + 2.0 * (real(0, 4) - real(1, 3)))
            gather(5, -2.0 * (imag(1, 4) + imag(3, 2)))
            gather(6, real(3, 3) - 2.0 * real(2, 4))
            gather(7, 2.0 * imag(3, 4))
            gather(8, real(4, 4))
        for n in range(9):
            acc_ref[n, p * ROWS : (p + 1) * ROWS] += weight * totals[n]

    @pl.when(j == count - 1)
    def _():
        norm = 1.0 / jnp.sum(all_weights_ref[...], axis=1, keepdims=True)
        for p in range(N_SRC):
            rows = slice(p * ROWS, (p + 1) * ROWS)
            planes = [acc_ref[n, rows] * norm for n in range(9)]
            top = planes[8]
            planes[0] = planes[0] - top * (1.0 / 128.0)
            planes[2] = planes[2] + top * 0.25
            planes[4] = planes[4] - top * 1.25
            planes[6] = planes[6] + top * 2.0
            out_ref[p] = jnp.concatenate(planes[:8], axis=0).astype(jnp.bfloat16)


def image_planes(spectra, shift, offset, weights, codes, levels):
    left, right = wave_tables()
    by_column, by_row, shape_x, shape_y = cell_tables()
    vmem = pl.BlockSpec(memory_space=pltpu.VMEM)
    smem = pl.BlockSpec(memory_space=pltpu.SMEM)
    hbm = pl.BlockSpec(memory_space=pl.ANY)
    count = spectra.shape[0]
    return pl.pallas_call(
        image_kernel,
        grid=(count,),
        out_shape=jax.ShapeDtypeStruct((N_SRC, PLANES * ROWS, COLS), jnp.bfloat16),
        in_specs=[
            smem,
            smem,
            smem,
            smem,
            vmem,
            vmem,
            vmem,
            vmem,
            vmem,
            vmem,
            pl.BlockSpec((1, 3, 2, WIN, WIN), lambda j: (j, 0, 0, 0, 0)),
            hbm,
            hbm,
        ],
        out_specs=vmem,
        scratch_shapes=[
            pltpu.VMEM((128, 2 * WIN), jnp.bfloat16),
            pltpu.VMEM((2 * WIN, 2 * COLS), jnp.bfloat16),
            pltpu.VMEM((2, 2 * CELLS, CELLS), jnp.float32),
            pltpu.VMEM((2 * WIN, 3 * TERMS * WIN), jnp.bfloat16),
            pltpu.VMEM((3 * TERMS * 64, 2 * WIN), jnp.bfloat16),
            pltpu.VMEM((3 * TERMS * 64, 2 * COLS), jnp.float32),
            pltpu.VMEM((9, 64, COLS), jnp.float32),
            pltpu.SemaphoreType.DMA((2,)),
        ],
        compiler_params=pltpu.CompilerParams(vmem_limit_bytes=48 << 20),
        name="image",
    )(
        shift,
        offset,
        levels,
        weights,
        weights.reshape(1, -1),
        codes,
        jnp.asarray(by_column),
        jnp.asarray(by_row),
        jnp.asarray(shape_x),
        jnp.asarray(shape_y),
        spectra,
        jnp.asarray(left, jnp.bfloat16),
        jnp.asarray(right, jnp.bfloat16),
    )


AROUND = [(dr, dc) for dr in (-1, 0, 1) for dc in (-1, 0, 1) if (dr, dc) != (0, 0)]


def bake_kernel(
    planes_ref,
    quench_ref,
    acid_out,
    quench_out,
    inhibit_out,
    arrived,
    own_planes,
    own_strip,
    own_quench_strip,
    near_planes,
    near_strips,
    near_quench,
    near_quench_strips,
    field,
    send_sems,
    recv_sems,
    near_send,
    near_recv,
    quench_send,
    quench_recv,
):
    src, tx, ty = lax.axis_index("src"), lax.axis_index("tx"), lax.axis_index("ty")
    place = src * N_TX + tx

    def device_at(dr, dc):
        row = lax.rem(place + dr + N_SRC * N_TX, N_SRC * N_TX)
        column = lax.rem(ty + dc + N_TY, N_TY)
        return (row // N_TX, lax.rem(row, N_TX), column)

    peers = [(lax.rem(src + d, N_SRC), tx, ty) for d in range(1, N_SRC)]
    around = [device_at(dr, dc) for dr, dc in AROUND]
    barrier = pltpu.get_barrier_semaphore()
    for device in peers + around:
        pl.semaphore_signal(barrier, inc=1, device_id=device, device_id_type=MESH)
    pl.semaphore_wait(barrier, len(peers) + len(around))

    exchange = []
    for d in range(1, N_SRC):
        copy = pltpu.make_async_remote_copy(
            src_ref=planes_ref.at[lax.rem(src + d, N_SRC)],
            dst_ref=arrived.at[d - 1],
            send_sem=send_sems.at[d - 1],
            recv_sem=recv_sems.at[d - 1],
            device_id=peers[d - 1],
            device_id_type=MESH,
        )
        copy.start()
        exchange.append(copy)

    lane = lax.broadcasted_iota(jnp.int32, (8, COLS), 1)
    group = lane // 16

    def packed(tiles):
        total = jnp.zeros((8, COLS), jnp.float32)
        for n, tile in enumerate(tiles):
            moved = pltpu.roll(tile, (8 + 16 * n) % COLS, 1)
            total = jnp.where(group == n, moved, total)
        return total

    def unpacked(merged, n):
        tile = pltpu.roll(merged, (COLS - 8 - 16 * n) % COLS, 1)
        return jnp.where((lane < 8) | (lane >= COLS - 8), tile, 0.0)

    first_half = lax.rem(lane, 16) < 8

    for k in range(2):
        own_quench_strip[k] = packed(
            [quench_ref[r, zh * 8 : zh * 8 + 8, :] for r in range(4 * k, 4 * k + 4) for zh in range(2)]
        )

    def send_around(whole, strip, near_whole, near_strip, sends, recvs):
        copies = []
        for i, (dr, dc) in enumerate(AROUND):
            if dc == 0:
                source, target = whole, near_whole.at[0 if dr == 1 else 1]
            else:
                slot = (1 - dr) * 2 + (0 if dc == 1 else 1)
                source, target = strip, near_strip.at[slot]
            copy = pltpu.make_async_remote_copy(
                src_ref=source,
                dst_ref=target,
                send_sem=sends.at[i],
                recv_sem=recvs.at[i],
                device_id=around[i],
                device_id_type=MESH,
            )
            copy.start()
            copies.append(copy)
        return copies

    quench_copies = send_around(
        quench_ref, own_quench_strip, near_quench, near_quench_strips, quench_send, quench_recv
    )

    total = planes_ref[src].astype(jnp.float32)
    for d in range(1, N_SRC):
        exchange[d - 1].wait_recv()
        total = total + arrived[d - 1].astype(jnp.float32)
    own_planes[...] = total
    own_strip[...] = packed([own_planes[n * 8 : n * 8 + 8, :] for n in range(PLANES)])
    plane_copies = send_around(
        own_planes, own_strip, near_planes, near_strips, near_send, near_recv
    )

    for copy in quench_copies:
        copy.wait_recv()
    for g in range(3):
        source = quench_ref if g == 1 else near_quench.at[0 if g == 0 else 1]
        for r in range(8):
            field[0, 1, g * 8 + r, :, 0:COLS] = source[r]
        for k in range(2):
            merged = jnp.where(
                first_half, near_quench_strips[2 * g, k], near_quench_strips[2 * g + 1, k]
            )
            for n in range(8):
                row, zh = 4 * k + n // 2, n % 2
                field[0, 1, g * 8 + row, zh * 8 : zh * 8 + 8, COLS : 2 * COLS] = unpacked(
                    merged, n
                )

    z_at = lax.broadcasted_iota(jnp.int32, (DEPTH, COLS), 0).astype(jnp.float32)
    tau = (z_at - 7.5) * (1.0 / 7.5)
    fading = jnp.exp(-ABSORB * z_at)

    def start_acid(g, get, side):
        for r in range(8):
            value = jnp.broadcast_to(get(PLANES - 1)[r : r + 1], (DEPTH, COLS))
            for n in range(PLANES - 2, -1, -1):
                value = value * tau + get(n)[r : r + 1]
            acid = 1.0 - jnp.exp(-value * fading)
            field[0, 0, g * 8 + r, :, side * COLS : (side + 1) * COLS] = acid

    start_acid(1, lambda n: own_planes[n * 8 : n * 8 + 8, :], 0)
    for copy in plane_copies:
        copy.wait_recv()
    for g in range(3):
        if g != 1:
            start_acid(g, lambda n: near_planes[0 if g == 0 else 1, n * 8 : n * 8 + 8, :], 0)
        merged = jnp.where(first_half, near_strips[2 * g], near_strips[2 * g + 1])
        tiles = [unpacked(merged, n) for n in range(PLANES)]
        start_acid(g, lambda n: tiles[n], 1)

    z_index = lax.broadcasted_iota(jnp.int32, (DEPTH, 2 * COLS), 0)

    def around_sum(slot, which, row):
        here = field[slot, which, row]
        beside = (
            field[slot, which, row - 1]
            + field[slot, which, row + 1]
            + pltpu.roll(here, 1, 1)
            + pltpu.roll(here, 2 * COLS - 1, 1)
        )
        above = jnp.where(z_index == 0, here, pltpu.roll(here, 1, 0))
        below = jnp.where(z_index == DEPTH - 1, here, pltpu.roll(here, DEPTH - 1, 0))
        return here, beside, above + below

    spent = [jnp.zeros((DEPTH, COLS), jnp.float32) for _ in range(ROWS)]
    for step in range(STEPS):
        old, new = step % 2, 1 - step % 2
        last = step == STEPS - 1
        for row in range(step + 1, 23 - step):
            a, a_beside, a_depth = around_sum(old, 0, row)
            q, q_beside, q_depth = around_sum(old, 1, row)
            reaction = 0.08 * a * q
            a_new = 0.1 * a + 0.2 * a_beside + 0.05 * a_depth - reaction
            q_new = 0.73 * q + 0.06 * q_beside + 0.015 * q_depth - reaction
            own = row - 8
            if 0 <= own < ROWS:
                spent[own] = spent[own] + a[:, :COLS]
            if last:
                acid_out[own] = a_new[:, :COLS]
                quench_out[own] = q_new[:, :COLS]
                inhibit_out[own] = jnp.exp(-0.25 * spent[own])
            else:
                field[new, 0, row] = a_new
                field[new, 1, row] = q_new

    for copy in exchange + quench_copies + plane_copies:
        copy.wait_send()


def baked(planes, quench):
    vmem = pl.BlockSpec(memory_space=pltpu.VMEM)
    tile = jax.ShapeDtypeStruct((ROWS, DEPTH, COLS), jnp.float32)
    dma = pltpu.SemaphoreType.DMA
    return pl.pallas_call(
        bake_kernel,
        out_shape=(tile, tile, tile),
        in_specs=[vmem, vmem],
        out_specs=(vmem, vmem, vmem),
        scratch_shapes=[
            pltpu.VMEM((N_SRC - 1, PLANES * ROWS, COLS), jnp.bfloat16),
            pltpu.VMEM((PLANES * ROWS, COLS), jnp.float32),
            pltpu.VMEM((8, COLS), jnp.float32),
            pltpu.VMEM((2, 8, COLS), jnp.float32),
            pltpu.VMEM((2, PLANES * ROWS, COLS), jnp.float32),
            pltpu.VMEM((6, 8, COLS), jnp.float32),
            pltpu.VMEM((2, ROWS, DEPTH, COLS), jnp.float32),
            pltpu.VMEM((6, 2, 8, COLS), jnp.float32),
            pltpu.VMEM((2, 2, 24, DEPTH, 2 * COLS), jnp.float32),
            dma((7,)),
            dma((7,)),
            dma((8,)),
            dma((8,)),
            dma((8,)),
            dma((8,)),
        ],
        compiler_params=pltpu.CompilerParams(
            collective_id=0, has_side_effects=True, vmem_limit_bytes=48 << 20
        ),
        name="bake",
    )(planes, quench)


def per_device(
    spectra, pupil_shift, window_offset, source_weight, mask_codes, levels, quench_start
):
    planes = image_planes(
        spectra, pupil_shift, window_offset, source_weight, mask_codes, levels
    )
    return baked(planes, quench_start)


def solution(mesh):
    in_specs = (
        P("src", None, None, None, None),
        P("src", None),
        P("src", None),
        P(),
        P(),
        P(),
        P(("src", "tx"), None, "ty"),
    )
    out_specs = (
        P(("src", "tx"), None, "ty"),
        P(("src", "tx"), None, "ty"),
        P(("src", "tx"), None, "ty"),
    )
    return jax.shard_map(
        per_device, mesh=mesh, in_specs=in_specs, out_specs=out_specs, check_vma=False
    )
```

profile of v0, /device:TPU:1, one launch (start us, length us, event | category | flops | bytes accessed | tf_op | source)
XLA Modules:
  0.0 50.2 jit_solution(1692229678213650862)
XLA Ops:
  0.6 0.8 %copy.16.shift_ref = s32[4,2]{1,0:T(4,128)S(1)} copy(s32[4,2]{0,1:T(2,128)} %param.14) | data formatting | bytes 64 | tf_op args[1]
  1.4 0.8 %copy.17.offset_ref = s32[4,2]{1,0:T(4,128)S(1)} copy(s32[4,2]{0,1:T(2,128)} %param.15) | data formatting | bytes 64 | tf_op args[2]
  2.2 0.0 copy-start
  2.2 1.2 %copy-done = bf16[4,512,256]{2,1,0:T(8,128)(2,1)S(1)} copy-done((bf16[4,512,256]{2,1,0:T(8,128)(2,1)S(1)}, bf16[4,512,256]{2,1,0:T(8,128)(2,1)}, u32[]{:S(2)}) %copy-start) | copy-done | bytes 1048600
  3.4 0.0 copy-start.1
  3.4 1.2 %copy-done.1 = bf16[8,128,512]{2,1,0:T(8,128)(2,1)S(1)} copy-done((bf16[8,128,512]{2,1,0:T(8,128)(2,1)S(1)}, bf16[8,128,512]{2,1,0:T(8,128)(2,1)}, u32[]{:S(2)}) %copy-start.1) | copy-done | bytes 1048600
  4.6 0.0 copy-start.2
  4.6 1.0 %copy-done.2 = f32[2,512,128]{2,1,0:T(8,128)S(1)} copy-done((f32[2,512,128]{2,1,0:T(8,128)S(1)}, f32[2,512,128]{2,1,0:T(8,128)}, u32[]{:S(2)}) %copy-start.2) | copy-done | bytes 524312
  5.7 0.0 copy-start.3
  5.7 0.9 %copy-done.3 = f32[256,256]{1,0:T(8,128)S(1)} copy-done((f32[256,256]{1,0:T(8,128)S(1)}, f32[256,256]{1,0:T(8,128)}, u32[]{:S(2)}) %copy-start.3) | copy-done | bytes 262168
  6.6 0.0 copy-start.4
  6.6 0.9 %copy-done.4 = f32[256,256]{1,0:T(8,128)S(1)} copy-done((f32[256,256]{1,0:T(8,128)S(1)}, f32[256,256]{1,0:T(8,128)}, u32[]{:S(2)}) %copy-start.4) | copy-done | bytes 262168
  7.6 0.0 copy-start.5
  7.6 0.8 %copy-done.5 = s32[128,128]{1,0:T(8,128)S(1)} copy-done((s32[128,128]{1,0:T(8,128)S(1)}, s32[128,128]{1,0:T(8,128)}, u32[]{:S(2)}) %copy-start.5) | copy-done | bytes 65560
  8.4 0.0 copy-start.7
  8.4 0.8 %copy-done.7 = f32[2,8,512]{2,1,0:T(8,128)S(1)} copy-done((f32[2,8,512]{2,1,0:T(8,128)S(1)}, f32[2,8,512]{2,1,0:T(8,128)}, u32[]{:S(2)}) %copy-start.7) | copy-done | bytes 32792
  9.2 0.0 copy-start.8
  9.2 0.7 %copy-done.8 = f32[32]{0:T(128)S(1)} copy-done((f32[32]{0:T(128)S(1)}, f32[32]{0:T(128)}, u32[]{:S(2)}) %copy-start.8) | copy-done | bytes 152
  9.8 0.0 copy-start.9
  9.8 0.7 %copy-done.9 = f32[2,4]{1,0:T(2,128)S(1)} copy-done((f32[2,4]{1,0:T(2,128)S(1)}, f32[2,4]{1,0:T(2,128)}, u32[]{:S(2)}) %copy-start.9) | copy-done | bytes 56
  10.5 0.0 copy-start.6
  10.5 13.4 %image.1.planes_ref = bf16[8,64,128]{2,1,0:T(8,128)(2,1)S(1)} custom-call(s32[4,2]{1,0:T(4,128)S(1)} %copy.16.shift_ref, s32[4,2]{1,0:T(4,128)S(1)} %copy.17.offset_ref, f32[2,4]{1,0:T(2,128)S(1)} %copy-done.9, f32[32]{0:T(128)S(1)} %copy-done.8, f32[1,32]{1,0:T(1,128)S(1)} %bitcast.1, s32[128,128]{1,0:T(8,128)S(1)} %copy-done.5, f32[256,256]{1,0:T(8,128)S(1)} %copy-done.4, ...), custom_call_target="tpu_custom_call" | custom-call | tf_op jit(solution)/shard_map/image/pallas_call | solution.py:278
  23.9 0.0 copy-done.6
  23.9 24.4 %bake.1 = (f32[8,16,128]{2,1,0:T(8,128)S(1)}, f32[8,16,128]{2,1,0:T(8,128)S(1)}, f32[8,16,128]{2,1,0:T(8,128)S(1)}) custom-call(bf16[8,64,128]{2,1,0:T(8,128)(2,1)S(1)} %image.1.planes_ref, f32[8,16,128]{2,1,0:T(8,128)S(1)} %copy-done.6), custom_call_target="tpu_custom_call" | custom-call | tf_op jit(solution)/shard_map/bake/pallas_call | solution.py:516
  48.3 0.6 %copy.21 = f32[8,16,128]{2,1,0:T(8,128)} copy(f32[8,16,128]{2,1,0:T(8,128)S(1)} %get-tuple-element.6) | data formatting | bytes 131072
  48.9 0.6 %copy.22 = f32[8,16,128]{2,1,0:T(8,128)} copy(f32[8,16,128]{2,1,0:T(8,128)S(1)} %get-tuple-element.7) | data formatting | bytes 131072
  49.5 0.6 %copy.23 = f32[8,16,128]{2,1,0:T(8,128)} copy(f32[8,16,128]{2,1,0:T(8,128)S(1)} %get-tuple-element.8) | data formatting | bytes 131072
Async XLA Ops:
  2.2 1.2 %copy-start = (bf16[4,512,256]{2,1,0:T(8,128)(2,1)S(1)}, bf16[4,512,256]{2,1,0:T(8,128)(2,1)}, u32[]{:S(2)}) copy-start(bf16[4,512,256]{2,1,0:T(8,128)(2,1)} %constant.17.clone.right_hbm) | copy-start | bytes 3145732
  3.4 1.2 %copy-start.1 = (bf16[8,128,512]{2,1,0:T(8,128)(2,1)S(1)}, bf16[8,128,512]{2,1,0:T(8,128)(2,1)}, u32[]{:S(2)}) copy-start(bf16[8,128,512]{2,1,0:T(8,128)(2,1)} %constant.16.clone.left_hbm) | copy-start | bytes 3145732
  4.6 1.0 %copy-start.2 = (f32[2,512,128]{2,1,0:T(8,128)S(1)}, f32[2,512,128]{2,1,0:T(8,128)}, u32[]{:S(2)}) copy-start(f32[2,512,128]{2,1,0:T(8,128)} %constant.14.clone.shape_x_ref) | copy-start | bytes 1572868
  5.7 0.9 %copy-start.3 = (f32[256,256]{1,0:T(8,128)S(1)}, f32[256,256]{1,0:T(8,128)}, u32[]{:S(2)}) copy-start(f32[256,256]{1,0:T(8,128)} %constant.13.clone.by_row_ref) | copy-start | bytes 786436
  6.6 0.9 %copy-start.4 = (f32[256,256]{1,0:T(8,128)S(1)}, f32[256,256]{1,0:T(8,128)}, u32[]{:S(2)}) copy-start(f32[256,256]{1,0:T(8,128)} %constant.12.clone.by_column_ref) | copy-start | bytes 786436
  7.6 0.8 %copy-start.5 = (s32[128,128]{1,0:T(8,128)S(1)}, s32[128,128]{1,0:T(8,128)}, u32[]{:S(2)}) copy-start(s32[128,128]{1,0:T(8,128)} %codes_ref.1) | copy-start | bytes 196612
  8.4 0.8 %copy-start.7 = (f32[2,8,512]{2,1,0:T(8,128)S(1)}, f32[2,8,512]{2,1,0:T(8,128)}, u32[]{:S(2)}) copy-start(f32[2,8,512]{2,1,0:T(8,128)} %constant.15.clone.shape_y_ref) | copy-start | bytes 98308
  9.2 0.7 %copy-start.8 = (f32[32]{0:T(128)S(1)}, f32[32]{0:T(128)}, u32[]{:S(2)}) copy-start(f32[32]{0:T(128)} %weight_ref.1) | copy-start | bytes 388
  9.8 0.7 %copy-start.9 = (f32[2,4]{1,0:T(2,128)S(1)}, f32[2,4]{1,0:T(2,128)}, u32[]{:S(2)}) copy-start(f32[2,4]{1,0:T(2,128)} %levels_ref.1) | copy-start | bytes 100
  10.5 13.4 %copy-start.6 = (f32[8,16,128]{2,1,0:T(8,128)S(1)}, f32[8,16,128]{2,1,0:T(8,128)}, u32[]{:S(2)}) copy-start(f32[8,16,128]{2,1,0:T(8,128)} %quench_ref.1) | copy-start | bytes 196612
where the time goes:
time: 50.6 us; the launch traced here: 50.2 us
  Pallas kernels  37.8 us (75%)
  local copies, waits for them, and re-layouts  11.7 us (23%)
  between operations  0.67 us (1%)
    pallas_call x1, Pallas kernels, baked(): pl.pallas_call(bake_kernel, out_shape=(tile, tile, tile), in_specs=[vmem,...  24.4 us
    pallas_call x1, Pallas kernels, image_planes(): pl.pallas_call(image_kernel, grid=(count,), out_shape=jax.ShapeDtypeStruc...  13.4 us
    unnamed x25, local copies, waits for them, and re-layouts  11.7 us

commit v1 on v0

v1 whole, which is shorter than its diff:
```python
import functools
import math

import jax
import jax.numpy as jnp
import numpy as np
from jax import lax
from jax.experimental import pallas as pl
from jax.experimental.pallas import tpu as pltpu
from jax.sharding import PartitionSpec as P

RADIUS = 124
CELL = 4
STEPS = 8
NX = 512
NY = 512
WIN = 256
DEPTH = 16
N_SRC, N_TX, N_TY = 8, 8, 4
ROWS, COLS = 8, 128
CELLS = 128

TWO_PI = 2.0 * math.pi
NUM_AP = 0.33
DZ_WAVE = 0.148
ABSORB = 0.05

HALF = math.pi * DZ_WAVE * (1.0 - math.sqrt(1.0 - NUM_AP * NUM_AP))
REACH = HALF * 7.5
TERMS = 5
BLOCKS = 16
REACH_OFF = 3
PLANES = 8
MESH = pl.DeviceIdType.MESH


def fit(function, powers, reach):
    nodes = np.cos((2 * np.arange(400) + 1) * np.pi / 800)
    basis = np.stack([nodes**k for k in powers], 1)
    sides = np.linalg.lstsq(basis, function(reach * nodes), rcond=None)[0]
    return [float(v) for v in sides]


EVEN = fit(np.cos, (0, 2, 4), REACH)
ODD = fit(np.sin, (1, 3), REACH)
SCALE = [EVEN[0], ODD[0], -EVEN[1], -ODD[1], EVEN[2]]


def wave_tables():
    u = np.arange(WIN)
    left = np.zeros((N_TX, 2, N_SRC * ROWS, WIN))
    for tx in range(N_TX):
        local = np.arange(N_SRC * ROWS)
        x = (local // ROWS * N_TX + tx) * ROWS + local % ROWS
        angle = TWO_PI / NX * ((x[:, None] * (u[None, :] - WIN // 2)) % NX)
        c, s = np.cos(angle), np.sin(angle)
        left[tx] = np.stack([c, s])
    right = np.zeros((N_TY, 2, WIN, COLS))
    for ty in range(N_TY):
        y = ty * COLS + np.arange(COLS)
        angle = TWO_PI / NY * ((y[None, :] * (u[:, None] - WIN // 2)) % NY)
        c, s = np.cos(angle), np.sin(angle)
        right[ty] = np.stack([c, s])
    return left, right


def turn_tables():
    fx = np.arange(WIN + 8) - WIN // 2 - REACH_OFF
    fy = np.arange(WIN + 128) - WIN // 2 - REACH_OFF
    radial = fx[:, None] ** 2 + fy[None, :] ** 2
    limit = RADIUS * RADIUS
    axial = np.sqrt(1.0 - (NUM_AP / RADIUS) ** 2 * np.minimum(radial, limit))
    w = TWO_PI * DZ_WAVE * (axial - 1.0) / HALF + 1.0
    inside = radial <= limit
    turn = 8.0 * HALF * w
    table = np.stack([w, np.cos(turn) * inside, np.sin(turn) * inside])
    return np.stack(np.split(table, 3, axis=2), 1).astype(np.float32)


def cell_tables():
    a = np.arange(CELLS)
    angle = TWO_PI / CELLS * ((a[:, None] * a[None, :]) % CELLS)
    c, s = np.cos(angle), np.sin(angle)
    cell_waves = np.stack([c, s])
    orders = np.arange(NX) - NX // 2
    phase = TWO_PI / NX * ((orders[:, None] * np.arange(CELL)[None, :]) % NX)
    shape_re = np.cos(phase).sum(1) / NX
    shape_im = -np.sin(phase).sum(1) / NX
    shape = np.stack([shape_re, shape_im])
    shape_x = np.broadcast_to(shape[:, :, None], (2, NX, 128))
    shape_y = np.broadcast_to(shape[:, None, :], (2, 8, NY))
    return (
        cell_waves.astype(np.float32),
        shape_x.astype(np.float32),
        shape_y.astype(np.float32),
    )


def exact(left, right):
    return jnp.dot(
        left, right, precision=lax.Precision.HIGHEST, preferred_element_type=jnp.float32
    )


AROUND = [(dr, dc) for dr in (-1, 0, 1) for dc in (-1, 0, 1) if (dr, dc) != (0, 0)]


def image_kernel(
    shift_hbm,
    offset_hbm,
    weight_hbm,
    levels_hbm,
    codes_hbm,
    cell_waves_hbm,
    shape_x_hbm,
    shape_y_hbm,
    turn_hbm,
    left_hbm,
    right_hbm,
    spectra_hbm,
    quench_hbm,
    field,
    shift_ref,
    offset_ref,
    weight_ref,
    levels_ref,
    codes_ref,
    cell_waves_ref,
    shape_x_ref,
    shape_y_ref,
    turn_ref,
    left_in,
    right_in,
    left_ref,
    right_ref,
    spectra_ref,
    quench_ref,
    cells_ref,
    operand_a,
    operand_b,
    half_ref,
    wave_ref,
    acc_ref,
    planes_ref,
    arrived,
    own_planes,
    own_strip,
    own_quench_strip,
    near_planes,
    near_strips,
    near_quench,
    near_quench_strips,
    load_sems,
    spectra_sems,
    send_sems,
    recv_sems,
    near_send,
    near_recv,
    quench_send,
    quench_recv,
):
    src, tx, ty = lax.axis_index("src"), lax.axis_index("tx"), lax.axis_index("ty")
    place = src * N_TX + tx

    def device_at(dr, dc):
        row = lax.rem(place + dr + N_SRC * N_TX, N_SRC * N_TX)
        column = lax.rem(ty + dc + N_TY, N_TY)
        return (row // N_TX, lax.rem(row, N_TX), column)

    peers = [(lax.rem(src + d, N_SRC), tx, ty) for d in range(1, N_SRC)]
    around = [device_at(dr, dc) for dr, dc in AROUND]

    loads = {}
    pairs = [
        ("codes", codes_hbm, codes_ref),
        ("levels", levels_hbm, levels_ref),
        ("cell", cell_waves_hbm, cell_waves_ref),
        ("shift", shift_hbm, shift_ref),
        ("offset", offset_hbm, offset_ref),
        ("weight", weight_hbm, weight_ref),
        ("shape_x", shape_x_hbm, shape_x_ref),
        ("shape_y", shape_y_hbm, shape_y_ref),
        ("turn", turn_hbm, turn_ref),
        ("left", left_hbm.at[tx], left_in),
        ("right", right_hbm.at[ty], right_in),
        ("quench", quench_hbm, quench_ref),
    ]
    count = spectra_hbm.shape[0]
    spectra_loads = [
        pltpu.make_async_copy(spectra_hbm.at[j], spectra_ref.at[j], spectra_sems.at[j])
        for j in range(count)
    ]
    for i, (name, source, target) in enumerate(pairs):
        loads[name] = pltpu.make_async_copy(source, target, load_sems.at[i])
        loads[name].start()
        if name == "turn":
            spectra_loads[0].start()
    for copy in spectra_loads[1:]:
        copy.start()

    barrier = pltpu.get_barrier_semaphore()
    for device in peers + around:
        pl.semaphore_signal(barrier, inc=1, device_id=device, device_id_type=MESH)

    for name in ("codes", "levels", "cell"):
        loads[name].wait()
    codes = codes_ref[...]
    parts = []
    for part in range(2):
        grid = jnp.full(codes.shape, levels_ref[part, 3], jnp.float32)
        for level in range(3):
            grid = jnp.where(codes == level, levels_ref[part, level], grid)
        parts.append(grid)
    c, s = cell_waves_ref[0], cell_waves_ref[1]
    by_column = jnp.concatenate(
        [jnp.concatenate([c, -s], axis=1), jnp.concatenate([s, c], axis=1)], axis=0
    )
    by_row = jnp.concatenate(
        [jnp.concatenate([c, s], axis=1), jnp.concatenate([-s, c], axis=1)], axis=0
    )
    across = exact(jnp.concatenate(parts, axis=1), by_column)
    both = jnp.concatenate([across[:, :CELLS], across[:, CELLS:]], axis=0)
    full = exact(by_row, both)
    for part in range(2):
        piece = full[part * CELLS : (part + 1) * CELLS]
        cells_ref[part, 0:CELLS] = piece
        cells_ref[part, CELLS : 2 * CELLS] = piece
    operand_a[BLOCKS - 1] = jnp.zeros((2 * WIN, WIN), jnp.bfloat16)
    operand_b[BLOCKS - 1] = jnp.zeros((2 * WIN, WIN), jnp.bfloat16)
    half_ref[...] = jnp.zeros_like(half_ref)
    for name in ("shift", "offset", "weight", "shape_x", "shape_y", "turn", "left", "right"):
        loads[name].wait()

    rows = N_SRC * ROWS
    left_ref[0:rows, 0:WIN] = left_in[0]
    left_ref[0:rows, WIN : 2 * WIN] = -left_in[1]
    left_ref[rows : 2 * rows, 0:WIN] = left_in[1]
    left_ref[rows : 2 * rows, WIN : 2 * WIN] = left_in[0]
    right_ref[0:WIN, 0:COLS] = right_in[0]
    right_ref[0:WIN, COLS : 2 * COLS] = right_in[1]
    right_ref[WIN : 2 * WIN, 0:COLS] = -right_in[1]
    right_ref[WIN : 2 * WIN, COLS : 2 * COLS] = right_in[0]

    total_weight = weight_ref[0]
    for k in range(1, weight_ref.shape[0]):
        total_weight = total_weight + weight_ref[k]
    norm = 1.0 / jnp.full((1, COLS), total_weight, jnp.float32)

    def builder(j, operand):
        spectra_loads[j].wait()
        off_x, off_y = offset_ref[0, j], offset_ref[1, j]
        start_x = off_x - shift_ref[0, j] - WIN // 2 + NX // 2
        start_y = off_y - shift_ref[1, j] - WIN // 2 + NY // 2
        cell_x = lax.rem(start_x, CELLS)
        roll_y = lax.rem(2 * CELLS - lax.rem(start_y, CELLS), CELLS)
        turn_x = off_x + REACH_OFF
        turn_y = lax.rem(WIN + 128 - (off_y + REACH_OFF), WIN + 128)
        shape_y = [
            pltpu.roll(shape_y_ref[part], NY - start_y, 1)[:, :WIN] for part in range(2)
        ]
        y_re = jnp.concatenate([shape_y[0]] * 2, axis=0)
        y_im = jnp.concatenate([shape_y[1]] * 2, axis=0)

        def build(step):
            at = pl.multiple_of(step * 16, 16)
            cell_at = lax.rem(cell_x + at, CELLS)
            g_re = pltpu.roll(cells_ref[0, pl.ds(cell_at, 16), :], roll_y, 1)
            g_im = pltpu.roll(cells_ref[1, pl.ds(cell_at, 16), :], roll_y, 1)
            x_re = shape_x_ref[0, pl.ds(start_x + at, 16), :]
            x_im = shape_x_ref[1, pl.ds(start_x + at, 16), :]
            gx_re = g_re * x_re - g_im * x_im
            gx_im = g_re * x_im + g_im * x_re
            gx_re = jnp.concatenate([gx_re, gx_re], axis=1)
            gx_im = jnp.concatenate([gx_im, gx_im], axis=1)
            thin_re = gx_re * y_re - gx_im * y_im
            thin_im = gx_re * y_im + gx_im * y_re
            w, turn_re, turn_im = (
                pltpu.roll(
                    jnp.concatenate(
                        [turn_ref[k, t, pl.ds(turn_x + at, 16), :] for t in range(3)], axis=1
                    ),
                    turn_y,
                    1,
                )[:, :WIN]
                for k in range(3)
            )
            w = w.astype(jnp.bfloat16)
            h_re = thin_re * turn_re - thin_im * turn_im
            h_im = thin_re * turn_im + thin_im * turn_re
            for c in range(3):
                f_re = spectra_ref[j, c, 0, pl.ds(at, 16), :].astype(jnp.float32)
                f_im = spectra_ref[j, c, 1, pl.ds(at, 16), :].astype(jnp.float32)
                s_re = (f_re * h_re - f_im * h_im).astype(jnp.bfloat16)
                s_im = (f_re * h_im + f_im * h_re).astype(jnp.bfloat16)
                for n in range(TERMS):
                    operand[c * TERMS + n, pl.ds(at, 16), :] = s_re
                    operand[c * TERMS + n, pl.ds(WIN + at, 16), :] = s_im
                    if n < TERMS - 1:
                        s_re = s_re * w
                        s_im = s_im * w

        return build

    def transform(quad, operand, store):
        parity = lax.rem(quad, 2)
        before = pl.multiple_of(lax.rem(quad + 3, 4) * 256, 256)
        wave_ref[pl.ds(before, 256), :] = jnp.dot(
            half_ref[1 - parity], right_ref[...], preferred_element_type=jnp.float32
        )
        for b in range(4):
            halves = jnp.dot(
                left_ref[...], operand[quad * 4 + b], preferred_element_type=jnp.float32
            ).astype(jnp.bfloat16)
            half_ref[parity, b * 64 : (b + 1) * 64, 0:WIN] = halves[0:64]
            half_ref[parity, b * 64 : (b + 1) * 64, WIN : 2 * WIN] = halves[64:128]
            if store is not None:
                store(quad * 4 + b)

    def gather(j):
        wave_ref[768:1024, :] = jnp.dot(
            half_ref[1], right_ref[...], preferred_element_type=jnp.float32
        )
        weight = weight_ref[src * count + j] * norm
        for p in range(N_SRC):
            totals = [None] * 9

            def add(n, value):
                totals[n] = value if totals[n] is None else totals[n] + value

            for c in range(3):
                re, im = [], []
                for n in range(TERMS):
                    base = (c * TERMS + n) * 64 + p * ROWS
                    re.append(wave_ref[base : base + ROWS, 0:COLS] * SCALE[n])
                    im.append(wave_ref[base : base + ROWS, COLS : 2 * COLS] * SCALE[n])

                def real(a, b):
                    return re[a] * re[b] + im[a] * im[b]

                def imag(a, b):
                    return im[a] * re[b] - re[a] * im[b]

                add(0, real(0, 0))
                add(1, -2.0 * imag(1, 0))
                add(2, real(1, 1) - 2.0 * real(0, 2))
                add(3, 2.0 * (imag(1, 2) + imag(3, 0)))
                add(4, real(2, 2) + 2.0 * (real(0, 4) - real(1, 3)))
                add(5, -2.0 * (imag(1, 4) + imag(3, 2)))
                add(6, real(3, 3) - 2.0 * real(2, 4))
                add(7, 2.0 * imag(3, 4))
                add(8, real(4, 4))
            planes = [weight * value for value in totals]
            planes[0] = planes[0] - planes[8] * (1.0 / 128.0)
            planes[2] = planes[2] + planes[8] * 0.25
            planes[4] = planes[4] - planes[8] * 1.25
            planes[6] = planes[6] + planes[8] * 2.0
            if j > 0:
                planes = [
                    planes[n] + acc_ref[p, n * ROWS : (n + 1) * ROWS, :] for n in range(PLANES)
                ]
            if j < count - 1:
                for n in range(PLANES):
                    acc_ref[p, n * ROWS : (n + 1) * ROWS, :] = planes[n]
            else:
                planes_ref[p] = jnp.concatenate(planes[:PLANES], axis=0).astype(jnp.bfloat16)

    operands = (operand_a, operand_b)
    build = builder(0, operands[0])

    @pl.loop(0, 4)
    def _(quad):
        for b in range(4):
            build(quad * 4 + b)

    for j in range(count):
        build = builder(j + 1, operands[(j + 1) % 2]) if j + 1 < count else None
        pl.loop(0, 4)(functools.partial(transform, operand=operands[j % 2], store=build))
        gather(j)

    pl.semaphore_wait(barrier, len(peers) + len(around))

    exchange = []
    for d in range(1, N_SRC):
        copy = pltpu.make_async_remote_copy(
            src_ref=planes_ref.at[lax.rem(src + d, N_SRC)],
            dst_ref=arrived.at[d - 1],
            send_sem=send_sems.at[d - 1],
            recv_sem=recv_sems.at[d - 1],
            device_id=peers[d - 1],
            device_id_type=MESH,
        )
        copy.start()
        exchange.append(copy)

    loads["quench"].wait()
    lane = lax.broadcasted_iota(jnp.int32, (8, COLS), 1)
    group = lane // 16

    def packed(tiles):
        total = jnp.zeros((8, COLS), jnp.float32)
        for n, tile in enumerate(tiles):
            moved = pltpu.roll(tile, (8 + 16 * n) % COLS, 1)
            total = jnp.where(group == n, moved, total)
        return total

    def unpacked(merged, n):
        tile = pltpu.roll(merged, (COLS - 8 - 16 * n) % COLS, 1)
        return jnp.where((lane < 8) | (lane >= COLS - 8), tile, 0.0)

    first_half = lax.rem(lane, 16) < 8

    for k in range(2):
        own_quench_strip[k] = packed(
            [quench_ref[r, zh * 8 : zh * 8 + 8, :] for r in range(4 * k, 4 * k + 4) for zh in range(2)]
        )

    def send_around(whole, strip, near_whole, near_strip, sends, recvs):
        copies = []
        for i, (dr, dc) in enumerate(AROUND):
            if dc == 0:
                source, target = whole, near_whole.at[0 if dr == 1 else 1]
            else:
                slot = (1 - dr) * 2 + (0 if dc == 1 else 1)
                source, target = strip, near_strip.at[slot]
            copy = pltpu.make_async_remote_copy(
                src_ref=source,
                dst_ref=target,
                send_sem=sends.at[i],
                recv_sem=recvs.at[i],
                device_id=around[i],
                device_id_type=MESH,
            )
            copy.start()
            copies.append(copy)
        return copies

    quench_copies = send_around(
        quench_ref, own_quench_strip, near_quench, near_quench_strips, quench_send, quench_recv
    )

    total = planes_ref[src].astype(jnp.float32)
    for d in range(1, N_SRC):
        exchange[d - 1].wait_recv()
        total = total + arrived[d - 1].astype(jnp.float32)
    own_planes[...] = total
    own_strip[...] = packed([own_planes[n * 8 : n * 8 + 8, :] for n in range(PLANES)])
    plane_copies = send_around(
        own_planes, own_strip, near_planes, near_strips, near_send, near_recv
    )

    for copy in quench_copies:
        copy.wait_recv()
    for g in range(3):
        source = quench_ref if g == 1 else near_quench.at[0 if g == 0 else 1]
        for r in range(8):
            field[1, g * 8 + r, :, 0:COLS] = source[r]
        for k in range(2):
            merged = jnp.where(
                first_half, near_quench_strips[2 * g, k], near_quench_strips[2 * g + 1, k]
            )
            for n in range(8):
                row, zh = 4 * k + n // 2, n % 2
                field[1, g * 8 + row, zh * 8 : zh * 8 + 8, COLS : 2 * COLS] = unpacked(
                    merged, n
                )

    z_at = lax.broadcasted_iota(jnp.int32, (DEPTH, COLS), 0).astype(jnp.float32)
    tau = (z_at - 7.5) * (1.0 / 7.5)
    fading = jnp.exp(-ABSORB * z_at)

    def start_acid(g, get, side):
        for r in range(8):
            value = jnp.broadcast_to(get(PLANES - 1)[r : r + 1], (DEPTH, COLS))
            for n in range(PLANES - 2, -1, -1):
                value = value * tau + get(n)[r : r + 1]
            acid = 1.0 - jnp.exp(-value * fading)
            field[0, g * 8 + r, :, side * COLS : (side + 1) * COLS] = acid

    start_acid(1, lambda n: own_planes[n * 8 : n * 8 + 8, :], 0)
    for copy in plane_copies:
        copy.wait_recv()
    for g in range(3):
        if g != 1:
            start_acid(g, lambda n: near_planes[0 if g == 0 else 1, n * 8 : n * 8 + 8, :], 0)
        merged = jnp.where(first_half, near_strips[2 * g], near_strips[2 * g + 1])
        tiles = [unpacked(merged, n) for n in range(PLANES)]
        start_acid(g, lambda n: tiles[n], 1)

    for copy in exchange + quench_copies + plane_copies:
        copy.wait_send()


def halo_field(spectra, shift, offset, weights, codes, levels, quench):
    left, right = wave_tables()
    cell_waves, shape_x, shape_y = cell_tables()
    turn = turn_tables()
    bf16, f32, dma = jnp.bfloat16, jnp.float32, pltpu.SemaphoreType.DMA
    vmem, smem = pltpu.VMEM, pltpu.SMEM
    count = spectra.shape[0]
    return pl.pallas_call(
        image_kernel,
        out_shape=jax.ShapeDtypeStruct((2, 3 * ROWS, DEPTH, 2 * COLS), f32),
        in_specs=[pl.BlockSpec(memory_space=pltpu.HBM)] * 13,
        out_specs=pl.BlockSpec(memory_space=pltpu.VMEM),
        scratch_shapes=[
            smem((2, count), jnp.int32),
            smem((2, count), jnp.int32),
            smem(weights.shape, f32),
            smem(levels.shape, f32),
            vmem(codes.shape, jnp.int32),
            vmem(cell_waves.shape, f32),
            vmem(shape_x.shape, f32),
            vmem(shape_y.shape, f32),
            vmem(turn.shape, f32),
            vmem(left.shape[1:], bf16),
            vmem(right.shape[1:], bf16),
            vmem((2 * N_SRC * ROWS, 2 * WIN), bf16),
            vmem((2 * WIN, 2 * COLS), bf16),
            vmem(spectra.shape, bf16),
            vmem(quench.shape, f32),
            vmem((2, 2 * CELLS, CELLS), f32),
            vmem((BLOCKS, 2 * WIN, WIN), bf16),
            vmem((BLOCKS, 2 * WIN, WIN), bf16),
            vmem((2, 256, 2 * WIN), bf16),
            vmem((BLOCKS * 64, 2 * COLS), f32),
            vmem((N_SRC, PLANES * ROWS, COLS), f32),
            vmem((N_SRC, PLANES * ROWS, COLS), bf16),
            vmem((N_SRC - 1, PLANES * ROWS, COLS), bf16),
            vmem((PLANES * ROWS, COLS), f32),
            vmem((8, COLS), f32),
            vmem((2, 8, COLS), f32),
            vmem((2, PLANES * ROWS, COLS), f32),
            vmem((6, 8, COLS), f32),
            vmem((2, ROWS, DEPTH, COLS), f32),
            vmem((6, 2, 8, COLS), f32),
            dma((12,)),
            dma((count,)),
            dma((7,)),
            dma((7,)),
            dma((8,)),
            dma((8,)),
            dma((8,)),
            dma((8,)),
        ],
        compiler_params=pltpu.CompilerParams(
            collective_id=0, has_side_effects=True, vmem_limit_bytes=40 << 20
        ),
        name="image",
    )(*(pltpu.with_memory_space_constraint(value, pltpu.HBM) for value in (
        shift.T,
        offset.T,
        weights,
        levels,
        codes,
        jnp.asarray(cell_waves),
        jnp.asarray(shape_x),
        jnp.asarray(shape_y),
        jnp.asarray(turn),
        jnp.asarray(left, bf16),
        jnp.asarray(right, bf16),
        spectra,
        quench,
    )))


def bake_kernel(start, acid_hbm, quench_hbm, inhibit_hbm, field, acid_out, quench_out, inhibit_out, sems):
    z_index = lax.broadcasted_iota(jnp.int32, (DEPTH, 2 * COLS), 0)

    def around_sum(held, which, row):
        here = held[which, row]
        beside = (
            held[which, row - 1]
            + held[which, row + 1]
            + pltpu.roll(here, 1, 1)
            + pltpu.roll(here, 2 * COLS - 1, 1)
        )
        above = jnp.where(z_index == 0, here, pltpu.roll(here, 1, 0))
        below = jnp.where(z_index == DEPTH - 1, here, pltpu.roll(here, DEPTH - 1, 0))
        return here, beside, above + below

    spent = [jnp.zeros((DEPTH, COLS), jnp.float32) for _ in range(ROWS)]
    for step in range(STEPS):
        old = start if step == 0 else field.at[step % 2]
        new = field.at[1 - step % 2]
        last = step == STEPS - 1
        for row in range(step + 1, 23 - step):
            a, a_beside, a_depth = around_sum(old, 0, row)
            q, q_beside, q_depth = around_sum(old, 1, row)
            reaction = 0.08 * a * q
            a_new = 0.1 * a + 0.2 * a_beside + 0.05 * a_depth - reaction
            q_new = 0.73 * q + 0.06 * q_beside + 0.015 * q_depth - reaction
            own = row - 8
            if 0 <= own < ROWS:
                spent[own] = spent[own] + a[:, :COLS]
            if last:
                acid_out[own] = a_new[:, :COLS]
                quench_out[own] = q_new[:, :COLS]
                inhibit_out[own] = jnp.exp(-0.25 * spent[own])
            else:
                new[0, row] = a_new
                new[1, row] = q_new

    copies = [
        pltpu.make_async_copy(source, target, sems.at[i])
        for i, (source, target) in enumerate(
            ((acid_out, acid_hbm), (quench_out, quench_hbm), (inhibit_out, inhibit_hbm))
        )
    ]
    for copy in copies:
        copy.start()
    for copy in copies:
        copy.wait()


def baked(start):
    tile = (ROWS, DEPTH, COLS)
    out = jax.ShapeDtypeStruct(tile, jnp.float32)
    return pl.pallas_call(
        bake_kernel,
        out_shape=(out, out, out),
        in_specs=[pl.BlockSpec(memory_space=pltpu.VMEM)],
        out_specs=(pl.BlockSpec(memory_space=pltpu.HBM),) * 3,
        scratch_shapes=[
            pltpu.VMEM((2, 2, 24, DEPTH, 2 * COLS), jnp.float32),
            pltpu.VMEM(tile, jnp.float32),
            pltpu.VMEM(tile, jnp.float32),
            pltpu.VMEM(tile, jnp.float32),
            pltpu.SemaphoreType.DMA((3,)),
        ],
        compiler_params=pltpu.CompilerParams(vmem_limit_bytes=16 << 20),
        name="bake",
    )(start)


def per_device(
    spectra, pupil_shift, window_offset, source_weight, mask_codes, levels, quench_start
):
    return baked(
        halo_field(
            spectra,
            pupil_shift,
            window_offset,
            source_weight,
            mask_codes,
            levels,
            quench_start,
        )
    )


def solution(mesh):
    in_specs = (
        P("src", None, None, None, None),
        P("src", None),
        P("src", None),
        P(),
        P(),
        P(),
        P(("src", "tx"), None, "ty"),
    )
    out_specs = (
        P(("src", "tx"), None, "ty"),
        P(("src", "tx"), None, "ty"),
        P(("src", "tx"), None, "ty"),
    )
    return jax.shard_map(
        per_device, mesh=mesh, in_specs=in_specs, out_specs=out_specs, check_vma=False
    )
```

time: 50.6 us -> 33.5 us (0.66)
  local copies, waits for them, and re-layouts: 11.7 us -> 0 us
  Pallas kernels: 37.8 us -> 32.8 us
    unnamed x25 -> x0, local copies, waits for them, and re-layouts: 11.7 us -> none
    pallas_call x2, Pallas kernels: 37.8 us -> 32.8 us  [the longest x1 29.8 us: halo_field(): pl.pallas_call(image_kernel, out_shape=jax.ShapeDtypeStruct((2, 3 * ROWS,...]
where the time goes in v1:
time: 33.5 us; the launch traced here: 33.4 us
  Pallas kernels  32.8 us (98%)
  between operations  0.64 us (2%)
    pallas_call x1, Pallas kernels, halo_field(): pl.pallas_call(image_kernel, out_shape=jax.ShapeDtypeStruct((2, 3 * ROWS,...  29.8 us
    pallas_call x1, Pallas kernels, baked(): pl.pallas_call(bake_kernel, out_shape=(out, out, out), in_specs=[pl.Block...  2.96 us

profile of v1, /device:TPU:1, one launch (start us, length us, event | category | flops | bytes accessed | tf_op | source)
XLA Modules:
  0.0 33.4 jit_solution(8202412498974214308)
XLA Ops:
  0.6 29.8 %image.1.start = f32[2,24,16,256]{3,2,1,0:T(8,128)S(1)} custom-call(s32[2,4]{1,0:T(2,128)} %bitcast.2, s32[2,4]{1,0:T(2,128)} %bitcast.3, f32[32]{0:T(128)} %weight_hbm.1, f32[2,4]{1,0:T(2,128)} %levels_hbm.1, s32[128,128]{1,0:T(8,128)} %codes_hbm.1, f32[2,128,128]{2,1,0:T(8,128)} %constant.12.clone.cell_waves_hbm, ...), custom_call_target="tpu_custom_call" | custom-call | tf_op jit(solution)/shard_map/image/pallas_call | solution.py:500
  30.5 3.0 %bake.1 = (f32[8,16,128]{2,1,0:T(8,128)}, f32[8,16,128]{2,1,0:T(8,128)}, f32[8,16,128]{2,1,0:T(8,128)}) custom-call(f32[2,24,16,256]{3,2,1,0:T(8,128)S(1)} %image.1.start), custom_call_target="tpu_custom_call" | custom-call | tf_op jit(solution)/shard_map/bake/pallas_call | solution.py:618

commit v2 on v1

--- a/solution.py
+++ b/solution.py
@@ -28,7 +28,7 @@
 HALF = math.pi * DZ_WAVE * (1.0 - math.sqrt(1.0 - NUM_AP * NUM_AP))
 REACH = HALF * 7.5
 TERMS = 5
-BLOCKS = 16
+EARLY = 0
 REACH_OFF = 3
 PLANES = 8
 MESH = pl.DeviceIdType.MESH
@@ -139,7 +139,8 @@
     operand_a,
     operand_b,
     half_ref,
-    wave_ref,
+    wave_a,
+    wave_b,
     acc_ref,
     planes_ref,
     arrived,
@@ -225,9 +226,6 @@
         piece = full[part * CELLS : (part + 1) * CELLS]
         cells_ref[part, 0:CELLS] = piece
         cells_ref[part, CELLS : 2 * CELLS] = piece
-    operand_a[BLOCKS - 1] = jnp.zeros((2 * WIN, WIN), jnp.bfloat16)
-    operand_b[BLOCKS - 1] = jnp.zeros((2 * WIN, WIN), jnp.bfloat16)
-    half_ref[...] = jnp.zeros_like(half_ref)
     for name in ("shift", "offset", "weight", "shape_x", "shape_y", "turn", "left", "right"):
         loads[name].wait()
 
@@ -254,15 +252,24 @@
         cell_x = lax.rem(start_x, CELLS)
         roll_y = lax.rem(2 * CELLS - lax.rem(start_y, CELLS), CELLS)
         turn_x = off_x + REACH_OFF
-        turn_y = lax.rem(WIN + 128 - (off_y + REACH_OFF), WIN + 128)
+        turn_y = lax.rem(COLS - (off_y + REACH_OFF), COLS)
         shape_y = [
             pltpu.roll(shape_y_ref[part], NY - start_y, 1)[:, :WIN] for part in range(2)
         ]
-        y_re = jnp.concatenate([shape_y[0]] * 2, axis=0)
-        y_im = jnp.concatenate([shape_y[1]] * 2, axis=0)
+        y_both = [jnp.concatenate([value] * 2, axis=0) for value in shape_y]
+
+        lane = lax.broadcasted_iota(jnp.int32, (16, COLS), 1)
+        kept = lane < COLS - (off_y + REACH_OFF)
+
+        def turned(k, at):
+            moved = [
+                pltpu.roll(turn_ref[k, t, pl.ds(turn_x + at, 16), :], turn_y, 1)
+                for t in range(3)
+            ]
+            return [jnp.where(kept, moved[t], moved[t + 1]) for t in range(2)]
 
         def build(step):
-            at = pl.multiple_of(step * 16, 16)
+            at = step * 16 if isinstance(step, int) else pl.multiple_of(step * 16, 16)
             cell_at = lax.rem(cell_x + at, CELLS)
             g_re = pltpu.roll(cells_ref[0, pl.ds(cell_at, 16), :], roll_y, 1)
             g_im = pltpu.roll(cells_ref[1, pl.ds(cell_at, 16), :], roll_y, 1)
@@ -270,21 +277,15 @@
             x_im = shape_x_ref[1, pl.ds(start_x + at, 16), :]
             gx_re = g_re * x_re - g_im * x_im
             gx_im = g_re * x_im + g_im * x_re
+            w_both, turn_re_both, turn_im_both = (turned(k, at) for k in range(3))
+            w = jnp.concatenate(w_both, axis=1).astype(jnp.bfloat16)
+            turn_re = jnp.concatenate(turn_re_both, axis=1)
+            turn_im = jnp.concatenate(turn_im_both, axis=1)
             gx_re = jnp.concatenate([gx_re, gx_re], axis=1)
             gx_im = jnp.concatenate([gx_im, gx_im], axis=1)
+            y_re, y_im = y_both
             thin_re = gx_re * y_re - gx_im * y_im
             thin_im = gx_re * y_im + gx_im * y_re
-            w, turn_re, turn_im = (
-                pltpu.roll(
-                    jnp.concatenate(
-                        [turn_ref[k, t, pl.ds(turn_x + at, 16), :] for t in range(3)], axis=1
-                    ),
-                    turn_y,
-                    1,
-                )[:, :WIN]
-                for k in range(3)
-            )
-            w = w.astype(jnp.bfloat16)
             h_re = thin_re * turn_re - thin_im * turn_im
             h_im = thin_re * turn_im + thin_im * turn_re
             for c in range(3):
@@ -301,98 +302,66 @@
 
         return build
 
-    def transform(quad, operand, store):
-        parity = lax.rem(quad, 2)
-        before = pl.multiple_of(lax.rem(quad + 3, 4) * 256, 256)
-        wave_ref[pl.ds(before, 256), :] = jnp.dot(
-            half_ref[1 - parity], right_ref[...], preferred_element_type=jnp.float32
+    def first(operand, block):
+        halves = jnp.dot(
+            left_ref[...], operand[block], preferred_element_type=jnp.float32
+        ).astype(jnp.bfloat16)
+        half_ref[block * 64 : (block + 1) * 64, 0:WIN] = halves[0:64]
+        half_ref[block * 64 : (block + 1) * 64, WIN : 2 * WIN] = halves[64:128]
+
+    def second(wave, c):
+        span = slice(c * TERMS * 64, (c + 1) * TERMS * 64)
+        wave[span, :] = jnp.dot(
+            half_ref[span, :], right_ref[...], preferred_element_type=jnp.float32
         )
-        for b in range(4):
-            halves = jnp.dot(
-                left_ref[...], operand[quad * 4 + b], preferred_element_type=jnp.float32
-            ).astype(jnp.bfloat16)
-            half_ref[parity, b * 64 : (b + 1) * 64, 0:WIN] = halves[0:64]
-            half_ref[parity, b * 64 : (b + 1) * 64, WIN : 2 * WIN] = halves[64:128]
-            if store is not None:
-                store(quad * 4 + b)
-
-    def gather(j):
-        wave_ref[768:1024, :] = jnp.dot(
-            half_ref[1], right_ref[...], preferred_element_type=jnp.float32
-        )
+
+    def gather(j, wave, p):
+        at = p * ROWS
+        if j == count - 1:
+            at = pl.multiple_of(at, ROWS)
         weight = weight_ref[src * count + j] * norm
-        for p in range(N_SRC):
-            totals = [None] * 9
-
-            def add(n, value):
-                totals[n] = value if totals[n] is None else totals[n] + value
-
-            for c in range(3):
-                re, im = [], []
-                for n in range(TERMS):
-                    base = (c * TERMS + n) * 64 + p * ROWS
-                    re.append(wave_ref[base : base + ROWS, 0:COLS] * SCALE[n])
-                    im.append(wave_ref[base : base + ROWS, COLS : 2 * COLS] * SCALE[n])
-
-                def real(a, b):
-                    return re[a] * re[b] + im[a] * im[b]
-
-                def imag(a, b):
-                    return im[a] * re[b] - re[a] * im[b]
-
-                add(0, real(0, 0))
-                add(1, -2.0 * imag(1, 0))
-                add(2, real(1, 1) - 2.0 * real(0, 2))
-                add(3, 2.0 * (imag(1, 2) + imag(3, 0)))
-                add(4, real(2, 2) + 2.0 * (real(0, 4) - real(1, 3)))
-                add(5, -2.0 * (imag(1, 4) + imag(3, 2)))
-                add(6, real(3, 3) - 2.0 * real(2, 4))
-                add(7, 2.0 * imag(3, 4))
-                add(8, real(4, 4))
-            planes = [weight * value for value in totals]
-            planes[0] = planes[0] - planes[8] * (1.0 / 128.0)
-            planes[2] = planes[2] + planes[8] * 0.25
-            planes[4] = planes[4] - planes[8] * 1.25
-            planes[6] = planes[6] + planes[8] * 2.0
-            if j > 0:
-                planes = [
-                    planes[n] + acc_ref[p, n * ROWS : (n + 1) * ROWS, :] for n in range(PLANES)
-                ]
-            if j < count - 1:
-                for n in range(PLANES):
-                    acc_ref[p, n * ROWS : (n + 1) * ROWS, :] = planes[n]
-            else:
-                planes_ref[p] = jnp.concatenate(planes[:PLANES], axis=0).astype(jnp.bfloat16)
-
-    operands = (operand_a, operand_b)
-    build = builder(0, operands[0])
-
-    @pl.loop(0, 4)
-    def _(quad):
-        for b in range(4):
-            build(quad * 4 + b)
-
-    for j in range(count):
-        build = builder(j + 1, operands[(j + 1) % 2]) if j + 1 < count else None
-        pl.loop(0, 4)(functools.partial(transform, operand=operands[j % 2], store=build))
-        gather(j)
-
-    pl.semaphore_wait(barrier, len(peers) + len(around))
-
-    exchange = []
-    for d in range(1, N_SRC):
-        copy = pltpu.make_async_remote_copy(
-            src_ref=planes_ref.at[lax.rem(src + d, N_SRC)],
-            dst_ref=arrived.at[d - 1],
-            send_sem=send_sems.at[d - 1],
-            recv_sem=recv_sems.at[d - 1],
-            device_id=peers[d - 1],
-            device_id_type=MESH,
-        )
-        copy.start()
-        exchange.append(copy)
-
-    loads["quench"].wait()
+        totals = [None] * 9
+
+        def add(n, value):
+            totals[n] = value if totals[n] is None else totals[n] + value
+
+        for c in range(3):
+            re, im = [], []
+            for n in range(TERMS):
+                rows = pl.ds((c * TERMS + n) * 64 + at, ROWS)
+                re.append(wave[rows, 0:COLS] * SCALE[n])
+                im.append(wave[rows, COLS : 2 * COLS] * SCALE[n])
+
+            def real(a, b):
+                return re[a] * re[b] + im[a] * im[b]
+
+            def imag(a, b):
+                return im[a] * re[b] - re[a] * im[b]
+
+            add(0, real(0, 0))
+            add(1, -2.0 * imag(1, 0))
+            add(2, real(1, 1) - 2.0 * real(0, 2))
+            add(3, 2.0 * (imag(1, 2) + imag(3, 0)))
+            add(4, real(2, 2) + 2.0 * (real(0, 4) - real(1, 3)))
+            add(5, -2.0 * (imag(1, 4) + imag(3, 2)))
+            add(6, real(3, 3) - 2.0 * real(2, 4))
+            add(7, 2.0 * imag(3, 4))
+            add(8, real(4, 4))
+        planes = [weight * value for value in totals]
+        planes[0] = planes[0] - planes[8] * (1.0 / 128.0)
+        planes[2] = planes[2] + planes[8] * 0.25
+        planes[4] = planes[4] - planes[8] * 1.25
+        planes[6] = planes[6] + planes[8] * 2.0
+        if j > 0:
+            planes = [
+                planes[n] + acc_ref[p, n * ROWS : (n + 1) * ROWS, :] for n in range(PLANES)
+            ]
+        if j < count - 1:
+            for n in range(PLANES):
+                acc_ref[p, n * ROWS : (n + 1) * ROWS, :] = planes[n]
+        else:
+            planes_ref[p] = jnp.concatenate(planes[:PLANES], axis=0).astype(jnp.bfloat16)
+
     lane = lax.broadcasted_iota(jnp.int32, (8, COLS), 1)
     group = lane // 16
 
@@ -408,11 +377,6 @@
         return jnp.where((lane < 8) | (lane >= COLS - 8), tile, 0.0)
 
     first_half = lax.rem(lane, 16) < 8
-
-    for k in range(2):
-        own_quench_strip[k] = packed(
-            [quench_ref[r, zh * 8 : zh * 8 + 8, :] for r in range(4 * k, 4 * k + 4) for zh in range(2)]
-        )
 
     def send_around(whole, strip, near_whole, near_strip, sends, recvs):
         copies = []
@@ -434,13 +398,57 @@
             copies.append(copy)
         return copies
 
-    quench_copies = send_around(
-        quench_ref, own_quench_strip, near_quench, near_quench_strips, quench_send, quench_recv
-    )
+    operands = (operand_a, operand_b)
+    waves = (wave_a, wave_b)
+    build = builder(0, operands[0])
+
+    @pl.loop(0, 4)
+    def _(quad):
+        for b in range(4):
+            build(quad * 4 + b)
+
+    for j in range(count):
+        build = builder(j + 1, operands[(j + 1) % 2]) if j + 1 < count else None
+        for step in range(WIN // 16):
+            if step < 3 * TERMS:
+                first(operands[j % 2], step)
+            if build is not None:
+                build(step)
+            if j > 0 and step % 2 == 0:
+                gather(j - 1, waves[(j - 1) % 2], step // 2)
+            if step in (5, 10, 15):
+                second(waves[j % 2], step // 5 - 1)
+        if j == EARLY:
+            pl.semaphore_wait(barrier, len(peers) + len(around))
+            loads["quench"].wait()
+            for k in range(2):
+                own_quench_strip[k] = packed(
+                    [quench_ref[r, zh * 8 : zh * 8 + 8, :] for r in range(4 * k, 4 * k + 4) for zh in range(2)]
+                )
+
+            quench_copies = send_around(
+                quench_ref, own_quench_strip, near_quench, near_quench_strips, quench_send, quench_recv
+            )
+
+    exchange = []
+    for d in (4, 5, 3, 6, 2, 7, 1, 0):
+        peer = lax.rem(src + d, N_SRC)
+        gather(count - 1, waves[(count - 1) % 2], peer)
+        if d > 0:
+            copy = pltpu.make_async_remote_copy(
+                src_ref=planes_ref.at[peer],
+                dst_ref=arrived.at[d - 1],
+                send_sem=send_sems.at[d - 1],
+                recv_sem=recv_sems.at[d - 1],
+                device_id=peers[d - 1],
+                device_id_type=MESH,
+            )
+            copy.start()
+            exchange.append(copy)
 
     total = planes_ref[src].astype(jnp.float32)
     for d in range(1, N_SRC):
-        exchange[d - 1].wait_recv()
+        exchange[(6, 4, 2, 0, 1, 3, 5)[d - 1]].wait_recv()
         total = total + arrived[d - 1].astype(jnp.float32)
     own_planes[...] = total
     own_strip[...] = packed([own_planes[n * 8 : n * 8 + 8, :] for n in range(PLANES)])
@@ -519,10 +527,11 @@
             vmem(spectra.shape, bf16),
             vmem(quench.shape, f32),
             vmem((2, 2 * CELLS, CELLS), f32),
-            vmem((BLOCKS, 2 * WIN, WIN), bf16),
-            vmem((BLOCKS, 2 * WIN, WIN), bf16),
-            vmem((2, 256, 2 * WIN), bf16),
-            vmem((BLOCKS * 64, 2 * COLS), f32),
+            vmem((3 * TERMS, 2 * WIN, WIN), bf16),
+            vmem((3 * TERMS, 2 * WIN, WIN), bf16),
+            vmem((3 * TERMS * 64, 2 * WIN), bf16),
+            vmem((3 * TERMS * 64, 2 * COLS), f32),
+            vmem((3 * TERMS * 64, 2 * COLS), f32),
             vmem((N_SRC, PLANES * ROWS, COLS), f32),
             vmem((N_SRC, PLANES * ROWS, COLS), bf16),
             vmem((N_SRC - 1, PLANES * ROWS, COLS), bf16),

time: 33.5 us -> 29.7 us (0.89)
  Pallas kernels: 32.8 us -> 28.9 us
    pallas_call x1, Pallas kernels: 29.8 us -> 26 us  [halo_field(): pl.pallas_call(image_kernel, out_shape=jax.ShapeDtypeStruct((2, 3 * ROWS,...]
where the time goes in v2:
time: 29.7 us; the launch traced here: 29.6 us
  Pallas kernels  28.9 us (97%)
  between operations  0.64 us (2%)
    pallas_call x1, Pallas kernels, halo_field(): pl.pallas_call(image_kernel, out_shape=jax.ShapeDtypeStruct((2, 3 * ROWS,...  26 us
    pallas_call x1, Pallas kernels, baked(): pl.pallas_call(bake_kernel, out_shape=(out, out, out), in_specs=[pl.Block...  2.96 us

profile of v2, /device:TPU:1, one launch (start us, length us, event | category | flops | bytes accessed | tf_op | source)
XLA Modules:
  0.0 29.6 jit_solution(16931790096426166886)
XLA Ops:
  0.6 26.0 %image.1.start = f32[2,24,16,256]{3,2,1,0:T(8,128)S(1)} custom-call(s32[2,4]{1,0:T(2,128)} %bitcast.2, s32[2,4]{1,0:T(2,128)} %bitcast.3, f32[32]{0:T(128)} %weight_hbm.1, f32[2,4]{1,0:T(2,128)} %levels_hbm.1, s32[128,128]{1,0:T(8,128)} %codes_hbm.1, f32[2,128,128]{2,1,0:T(8,128)} %constant.12.clone.cell_waves_hbm, ...), custom_call_target="tpu_custom_call" | custom-call | tf_op jit(solution)/shard_map/image/pallas_call | solution.py:508
  26.6 3.0 %bake.1 = (f32[8,16,128]{2,1,0:T(8,128)}, f32[8,16,128]{2,1,0:T(8,128)}, f32[8,16,128]{2,1,0:T(8,128)}) custom-call(f32[2,24,16,256]{3,2,1,0:T(8,128)S(1)} %image.1.start), custom_call_target="tpu_custom_call" | custom-call | tf_op jit(solution)/shard_map/bake/pallas_call | solution.py:627

commit v3 on v2

--- a/solution.py
+++ b/solution.py
@@ -24,13 +24,14 @@
 NUM_AP = 0.33
 DZ_WAVE = 0.148
 ABSORB = 0.05
+NEUTRAL = 0.08
 
 HALF = math.pi * DZ_WAVE * (1.0 - math.sqrt(1.0 - NUM_AP * NUM_AP))
 REACH = HALF * 7.5
 TERMS = 5
 EARLY = 0
 REACH_OFF = 3
-PLANES = 8
+PLANES = 6
 MESH = pl.DeviceIdType.MESH
 
 
@@ -81,7 +82,9 @@
     a = np.arange(CELLS)
     angle = TWO_PI / CELLS * ((a[:, None] * a[None, :]) % CELLS)
     c, s = np.cos(angle), np.sin(angle)
-    cell_waves = np.stack([c, s])
+    waves = np.stack([c, s]).astype(np.float32)
+    high = waves.astype(jnp.bfloat16).astype(np.float32)
+    cell_waves = np.stack([high, waves - high])
     orders = np.arange(NX) - NX // 2
     phase = TWO_PI / NX * ((orders[:, None] * np.arange(CELL)[None, :]) % NX)
     shape_re = np.cos(phase).sum(1) / NX
@@ -90,15 +93,9 @@
     shape_x = np.broadcast_to(shape[:, :, None], (2, NX, 128))
     shape_y = np.broadcast_to(shape[:, None, :], (2, 8, NY))
     return (
-        cell_waves.astype(np.float32),
+        cell_waves,
         shape_x.astype(np.float32),
         shape_y.astype(np.float32),
-    )
-
-
-def exact(left, right):
-    return jnp.dot(
-        left, right, precision=lax.Precision.HIGHEST, preferred_element_type=jnp.float32
     )
 
 
@@ -212,16 +209,37 @@
         for level in range(3):
             grid = jnp.where(codes == level, levels_ref[part, level], grid)
         parts.append(grid)
-    c, s = cell_waves_ref[0], cell_waves_ref[1]
-    by_column = jnp.concatenate(
-        [jnp.concatenate([c, -s], axis=1), jnp.concatenate([s, c], axis=1)], axis=0
+    by_column, by_row = [], []
+    for part in range(2):
+        c, s = cell_waves_ref[part, 0], cell_waves_ref[part, 1]
+        by_column.append(
+            jnp.concatenate(
+                [jnp.concatenate([c, -s], axis=1), jnp.concatenate([s, c], axis=1)], axis=0
+            )
+        )
+        by_row.append(
+            jnp.concatenate(
+                [jnp.concatenate([c, s], axis=1), jnp.concatenate([-s, c], axis=1)], axis=0
+            )
+        )
+    by_column = jnp.concatenate([by_column[0], by_column[0], by_column[1]], axis=0)
+    by_row = jnp.concatenate([by_row[0], by_row[0], by_row[1]], axis=1)
+    grid = jnp.concatenate(parts, axis=1)
+    high = grid.astype(jnp.bfloat16)
+    low = (grid - high.astype(jnp.float32)).astype(jnp.bfloat16)
+    across = jnp.dot(
+        jnp.concatenate([high, low, high], axis=1),
+        by_column,
+        preferred_element_type=jnp.float32,
     )
-    by_row = jnp.concatenate(
-        [jnp.concatenate([c, s], axis=1), jnp.concatenate([-s, c], axis=1)], axis=0
+    both = jnp.concatenate([across[:, :CELLS], across[:, CELLS:]], axis=0)
+    high = both.astype(jnp.bfloat16)
+    low = (both - high.astype(jnp.float32)).astype(jnp.bfloat16)
+    full = jnp.dot(
+        by_row,
+        jnp.concatenate([high, low, high], axis=0),
+        preferred_element_type=jnp.float32,
     )
-    across = exact(jnp.concatenate(parts, axis=1), by_column)
-    both = jnp.concatenate([across[:, :CELLS], across[:, CELLS:]], axis=0)
-    full = exact(by_row, both)
     for part in range(2):
         piece = full[part * CELLS : (part + 1) * CELLS]
         cells_ref[part, 0:CELLS] = piece
@@ -242,7 +260,7 @@
     total_weight = weight_ref[0]
     for k in range(1, weight_ref.shape[0]):
         total_weight = total_weight + weight_ref[k]
-    norm = 1.0 / jnp.full((1, COLS), total_weight, jnp.float32)
+    norm = 1.0 / jnp.full((ROWS, COLS), total_weight, jnp.float32)
 
     def builder(j, operand):
         spectra_loads[j].wait()
@@ -320,38 +338,37 @@
         if j == count - 1:
             at = pl.multiple_of(at, ROWS)
         weight = weight_ref[src * count + j] * norm
-        totals = [None] * 9
-
-        def add(n, value):
-            totals[n] = value if totals[n] is None else totals[n] + value
-
+        real = ((0, 0), (1, 1), (0, 2), (2, 2), (0, 4), (1, 3), (3, 3), (2, 4), (4, 4))
+        imag = ((1, 0), (1, 2), (3, 0), (1, 4), (3, 2), (3, 4))
+        total = {}
         for c in range(3):
             re, im = [], []
             for n in range(TERMS):
                 rows = pl.ds((c * TERMS + n) * 64 + at, ROWS)
-                re.append(wave[rows, 0:COLS] * SCALE[n])
-                im.append(wave[rows, COLS : 2 * COLS] * SCALE[n])
-
-            def real(a, b):
-                return re[a] * re[b] + im[a] * im[b]
-
-            def imag(a, b):
-                return im[a] * re[b] - re[a] * im[b]
-
-            add(0, real(0, 0))
-            add(1, -2.0 * imag(1, 0))
-            add(2, real(1, 1) - 2.0 * real(0, 2))
-            add(3, 2.0 * (imag(1, 2) + imag(3, 0)))
-            add(4, real(2, 2) + 2.0 * (real(0, 4) - real(1, 3)))
-            add(5, -2.0 * (imag(1, 4) + imag(3, 2)))
-            add(6, real(3, 3) - 2.0 * real(2, 4))
-            add(7, 2.0 * imag(3, 4))
-            add(8, real(4, 4))
-        planes = [weight * value for value in totals]
-        planes[0] = planes[0] - planes[8] * (1.0 / 128.0)
-        planes[2] = planes[2] + planes[8] * 0.25
-        planes[4] = planes[4] - planes[8] * 1.25
-        planes[6] = planes[6] + planes[8] * 2.0
+                re.append(wave[rows, 0:COLS])
+                im.append(wave[rows, COLS : 2 * COLS])
+            for a, b in real:
+                value = re[a] * re[b] + im[a] * im[b]
+                total[a, b] = value if c == 0 else total[a, b] + value
+            for a, b in imag:
+                value = im[a] * re[b] - re[a] * im[b]
+                total[-a - 1, b] = value if c == 0 else total[-a - 1, b] + value
+
+        def part(a, b, factor):
+            sign = a if a >= 0 else -a - 1
+            return total[a, b] * (weight * (factor * SCALE[sign] * SCALE[b]))
+
+        eighth = part(4, 4, 1.0)
+        seventh = part(-4, 4, 2.0)
+        sixth = part(3, 3, 1.0) + part(2, 4, -2.0) + 2.0 * eighth
+        planes = [
+            part(0, 0, 1.0) + sixth * (1.0 / 32.0) - eighth * (1.0 / 128.0),
+            part(-2, 0, -2.0) + seventh * (7.0 / 64.0),
+            part(1, 1, 1.0) + part(0, 2, -2.0) + eighth * 0.25 - sixth * 0.5625,
+            part(-2, 2, 2.0) + part(-4, 0, 2.0) - seventh * 0.875,
+            part(2, 2, 1.0) + part(0, 4, 2.0) + part(1, 3, -2.0) + sixth * 1.5 - eighth * 1.25,
+            part(-2, 4, -2.0) + part(-4, 2, -2.0) + seventh * 1.75,
+        ]
         if j > 0:
             planes = [
                 planes[n] + acc_ref[p, n * ROWS : (n + 1) * ROWS, :] for n in range(PLANES)
@@ -378,9 +395,11 @@
 
     first_half = lax.rem(lane, 16) < 8
 
-    def send_around(whole, strip, near_whole, near_strip, sends, recvs):
+    def send_around(rows, whole, strip, near_whole, near_strip, sends, recvs):
         copies = []
         for i, (dr, dc) in enumerate(AROUND):
+            if (dc == 0) != rows:
+                continue
             if dc == 0:
                 source, target = whole, near_whole.at[0 if dr == 1 else 1]
             else:
@@ -426,9 +445,17 @@
                     [quench_ref[r, zh * 8 : zh * 8 + 8, :] for r in range(4 * k, 4 * k + 4) for zh in range(2)]
                 )
 
-            quench_copies = send_around(
-                quench_ref, own_quench_strip, near_quench, near_quench_strips, quench_send, quench_recv
-            )
+            quench_copies = []
+            for rows in (True, False):
+                quench_copies += send_around(
+                    rows,
+                    quench_ref,
+                    own_quench_strip,
+                    near_quench,
+                    near_quench_strips,
+                    quench_send,
+                    quench_recv,
+                )
 
     exchange = []
     for d in (4, 5, 3, 6, 2, 7, 1, 0):
@@ -451,25 +478,26 @@
         exchange[(6, 4, 2, 0, 1, 3, 5)[d - 1]].wait_recv()
         total = total + arrived[d - 1].astype(jnp.float32)
     own_planes[...] = total
-    own_strip[...] = packed([own_planes[n * 8 : n * 8 + 8, :] for n in range(PLANES)])
-    plane_copies = send_around(
-        own_planes, own_strip, near_planes, near_strips, near_send, near_recv
-    )
+    near = (own_planes, own_strip, near_planes, near_strips, near_send, near_recv)
+    row_copies = send_around(True, *near)
+    own_strip[...] = packed([total[n * 8 : n * 8 + 8, :] for n in range(PLANES)])
+    strip_copies = send_around(False, *near)
+    plane_copies = row_copies + strip_copies
 
     for copy in quench_copies:
         copy.wait_recv()
     for g in range(3):
         source = quench_ref if g == 1 else near_quench.at[0 if g == 0 else 1]
         for r in range(8):
-            field[1, g * 8 + r, :, 0:COLS] = source[r]
+            field[1, g * 8 + r, :, 0:COLS] = NEUTRAL * source[r]
         for k in range(2):
             merged = jnp.where(
                 first_half, near_quench_strips[2 * g, k], near_quench_strips[2 * g + 1, k]
             )
             for n in range(8):
                 row, zh = 4 * k + n // 2, n % 2
-                field[1, g * 8 + row, zh * 8 : zh * 8 + 8, COLS : 2 * COLS] = unpacked(
-                    merged, n
+                field[1, g * 8 + row, zh * 8 : zh * 8 + 8, COLS : 2 * COLS] = (
+                    NEUTRAL * unpacked(merged, n)
                 )
 
     z_at = lax.broadcasted_iota(jnp.int32, (DEPTH, COLS), 0).astype(jnp.float32)
@@ -481,15 +509,17 @@
             value = jnp.broadcast_to(get(PLANES - 1)[r : r + 1], (DEPTH, COLS))
             for n in range(PLANES - 2, -1, -1):
                 value = value * tau + get(n)[r : r + 1]
-            acid = 1.0 - jnp.exp(-value * fading)
+            acid = NEUTRAL - NEUTRAL * jnp.exp(-value * fading)
             field[0, g * 8 + r, :, side * COLS : (side + 1) * COLS] = acid
 
     start_acid(1, lambda n: own_planes[n * 8 : n * 8 + 8, :], 0)
-    for copy in plane_copies:
+    for copy in row_copies:
+        copy.wait_recv()
+    for g in (0, 2):
+        start_acid(g, lambda n: near_planes[g // 2, n * 8 : n * 8 + 8, :], 0)
+    for copy in strip_copies:
         copy.wait_recv()
     for g in range(3):
-        if g != 1:
-            start_acid(g, lambda n: near_planes[0 if g == 0 else 1, n * 8 : n * 8 + 8, :], 0)
         merged = jnp.where(first_half, near_strips[2 * g], near_strips[2 * g + 1])
         tiles = [unpacked(merged, n) for n in range(PLANES)]
         start_acid(g, lambda n: tiles[n], 1)
@@ -516,7 +546,7 @@
             smem(weights.shape, f32),
             smem(levels.shape, f32),
             vmem(codes.shape, jnp.int32),
-            vmem(cell_waves.shape, f32),
+            vmem(cell_waves.shape, bf16),
             vmem(shape_x.shape, f32),
             vmem(shape_y.shape, f32),
             vmem(turn.shape, f32),
@@ -561,7 +591,7 @@
         weights,
         levels,
         codes,
-        jnp.asarray(cell_waves),
+        jnp.asarray(cell_waves, bf16),
         jnp.asarray(shape_x),
         jnp.asarray(shape_y),
         jnp.asarray(turn),
@@ -573,50 +603,78 @@
 
 
 def bake_kernel(start, acid_hbm, quench_hbm, inhibit_hbm, field, acid_out, quench_out, inhibit_out, sems):
-    z_index = lax.broadcasted_iota(jnp.int32, (DEPTH, 2 * COLS), 0)
-
-    def around_sum(held, which, row):
-        here = held[which, row]
-        beside = (
-            held[which, row - 1]
-            + held[which, row + 1]
-            + pltpu.roll(here, 1, 1)
-            + pltpu.roll(here, 2 * COLS - 1, 1)
-        )
-        above = jnp.where(z_index == 0, here, pltpu.roll(here, 1, 0))
-        below = jnp.where(z_index == DEPTH - 1, here, pltpu.roll(here, DEPTH - 1, 0))
-        return here, beside, above + below
-
-    spent = [jnp.zeros((DEPTH, COLS), jnp.float32) for _ in range(ROWS)]
+    shape = (DEPTH // 2, COLS)
+    lane = lax.broadcasted_iota(jnp.int32, shape, 1)
+    depth = lax.broadcasted_iota(jnp.int32, shape, 0)
+    first_lane, last_lane = lane == 0, lane == COLS - 1
+    top, bottom = depth == 0, depth == DEPTH // 2 - 1
+
+    def halves(held, which, row):
+        return [
+            [held[which, row, z : z + 8, t : t + COLS] for t in (0, COLS)] for z in (0, 8)
+        ]
+
+    def sums(held, which, row, sides):
+        before, here, after = (halves(held, which, row + k) for k in (-1, 0, 1))
+        out = []
+        for t in range(sides):
+            low, high = here[0][t], here[1][t]
+            low_up, high_up = pltpu.roll(low, 1, 0), pltpu.roll(high, 1, 0)
+            low_down, high_down = pltpu.roll(low, 7, 0), pltpu.roll(high, 7, 0)
+            along = (
+                jnp.where(top, low, low_up) + jnp.where(bottom, high_down, low_down),
+                jnp.where(top, low_up, high_up) + jnp.where(bottom, high, high_down),
+            )
+            for z in range(2):
+                mine, other = here[z][t], here[z][1 - t]
+                left = jnp.where(first_lane, pltpu.roll(other, 1, 1), pltpu.roll(mine, 1, 1))
+                right = jnp.where(
+                    last_lane, pltpu.roll(other, COLS - 1, 1), pltpu.roll(mine, COLS - 1, 1)
+                )
+                beside = (before[z][t] + after[z][t]) + (left + right)
+                out.append((z, t, mine, beside + 0.25 * along[z]))
+        return out
+
+    copies = []
+
+    def send(part):
+        rows = pl.ds(part * 4, 4)
+        for i, (source, target) in enumerate(
+            ((acid_out, acid_hbm), (quench_out, quench_hbm), (inhibit_out, inhibit_hbm))
+        ):
+            copy = pltpu.make_async_copy(
+                source.at[rows], target.at[rows], sems.at[part * 3 + i]
+            )
+            copy.start()
+            copies.append(copy)
+
+    spent = {}
     for step in range(STEPS):
         old = start if step == 0 else field.at[step % 2]
         new = field.at[1 - step % 2]
         last = step == STEPS - 1
         for row in range(step + 1, 23 - step):
-            a, a_beside, a_depth = around_sum(old, 0, row)
-            q, q_beside, q_depth = around_sum(old, 1, row)
-            reaction = 0.08 * a * q
-            a_new = 0.1 * a + 0.2 * a_beside + 0.05 * a_depth - reaction
-            q_new = 0.73 * q + 0.06 * q_beside + 0.015 * q_depth - reaction
+            sides = 1 if last or row in (step + 1, 22 - step) else 2
             own = row - 8
-            if 0 <= own < ROWS:
-                spent[own] = spent[own] + a[:, :COLS]
-            if last:
-                acid_out[own] = a_new[:, :COLS]
-                quench_out[own] = q_new[:, :COLS]
-                inhibit_out[own] = jnp.exp(-0.25 * spent[own])
-            else:
-                new[0, row] = a_new
-                new[1, row] = q_new
-
-    copies = [
-        pltpu.make_async_copy(source, target, sems.at[i])
-        for i, (source, target) in enumerate(
-            ((acid_out, acid_hbm), (quench_out, quench_hbm), (inhibit_out, inhibit_hbm))
-        )
-    ]
-    for copy in copies:
-        copy.start()
+            for (z, t, a, a_sum), (_, _, q, q_sum) in zip(
+                sums(old, 0, row, sides), sums(old, 1, row, sides)
+            ):
+                a_new = a * (0.1 - q) + 0.2 * a_sum
+                q_new = q * (0.73 - a) + 0.06 * q_sum
+                span = slice(z * 8, z * 8 + 8)
+                if 0 <= own < ROWS and t == 0:
+                    spent[own, z] = spent[own, z] + a if step else a
+                if last:
+                    acid_out[own, span] = a_new * (1.0 / NEUTRAL)
+                    quench_out[own, span] = q_new * (1.0 / NEUTRAL)
+                    inhibit_out[own, span] = jnp.exp((-0.25 / NEUTRAL) * spent[own, z])
+                else:
+                    lanes = slice(t * COLS, (t + 1) * COLS)
+                    new[0, row, span, lanes] = a_new
+                    new[1, row, span, lanes] = q_new
+            if last and own % 4 == 3:
+                send(own // 4)
+
     for copy in copies:
         copy.wait()
 
@@ -634,7 +692,7 @@
             pltpu.VMEM(tile, jnp.float32),
             pltpu.VMEM(tile, jnp.float32),
             pltpu.VMEM(tile, jnp.float32),
-            pltpu.SemaphoreType.DMA((3,)),
+            pltpu.SemaphoreType.DMA((6,)),
         ],
         compiler_params=pltpu.CompilerParams(vmem_limit_bytes=16 << 20),
         name="bake",

time: 29.7 us -> 29.3 us (0.987)
  Pallas kernels: 28.9 us -> 28.6 us
    pallas_call x1, Pallas kernels: 26 us -> 25.7 us  [halo_field(): pl.pallas_call(image_kernel, out_shape=jax.ShapeDtypeStruct((2, 3 * ROWS,...]
where the time goes in v3:
time: 29.3 us; the launch traced here: 29.2 us
  Pallas kernels  28.6 us (98%)
  between operations  0.64 us (2%)
    pallas_call x1, Pallas kernels, halo_field(): pl.pallas_call(image_kernel, out_shape=jax.ShapeDtypeStruct((2, 3 * ROWS,...  25.7 us
    pallas_call x1, Pallas kernels, baked(): pl.pallas_call(bake_kernel, out_shape=(out, out, out), in_specs=[pl.Block...  2.89 us

profile of v3, /device:TPU:1, one launch (start us, length us, event | category | flops | bytes accessed | tf_op | source)
XLA Modules:
  0.0 29.2 jit_solution(10552218812771668710)
XLA Ops:
  0.6 25.7 %image.1.start = f32[2,24,16,256]{3,2,1,0:T(8,128)S(1)} custom-call(s32[2,4]{1,0:T(2,128)} %bitcast.2, s32[2,4]{1,0:T(2,128)} %bitcast.3, f32[32]{0:T(128)} %weight_hbm.1, f32[2,4]{1,0:T(2,128)} %levels_hbm.1, s32[128,128]{1,0:T(8,128)} %codes_hbm.1, bf16[2,2,128,128]{3,2,1,0:T(8,128)(2,1)} %constant.12.clone.cell_waves_hbm, ...), custom_call_target="tpu_custom_call" | custom-call | tf_op jit(solution)/shard_map/image/pallas_call | solution.py:538
  26.3 2.9 %bake.1 = (f32[8,16,128]{2,1,0:T(8,128)}, f32[8,16,128]{2,1,0:T(8,128)}, f32[8,16,128]{2,1,0:T(8,128)}) custom-call(f32[2,24,16,256]{3,2,1,0:T(8,128)S(1)} %image.1.start), custom_call_target="tpu_custom_call" | custom-call | tf_op jit(solution)/shard_map/bake/pallas_call | solution.py:685

commit v4 on v3

--- a/solution.py
+++ b/solution.py
@@ -99,7 +99,7 @@
     )
 
 
-AROUND = [(dr, dc) for dr in (-1, 0, 1) for dc in (-1, 0, 1) if (dr, dc) != (0, 0)]
+AROUND = [(-1, -1), (-1, 1), (1, -1), (1, 1), (0, -1), (0, 1), (-1, 0), (1, 0)]
 
 
 def image_kernel(
@@ -421,10 +421,8 @@
     waves = (wave_a, wave_b)
     build = builder(0, operands[0])
 
-    @pl.loop(0, 4)
-    def _(quad):
-        for b in range(4):
-            build(quad * 4 + b)
+    for step in range(WIN // 16):
+        build(step)
 
     for j in range(count):
         build = builder(j + 1, operands[(j + 1) % 2]) if j + 1 < count else None
@@ -479,9 +477,9 @@
         total = total + arrived[d - 1].astype(jnp.float32)
     own_planes[...] = total
     near = (own_planes, own_strip, near_planes, near_strips, near_send, near_recv)
-    row_copies = send_around(True, *near)
     own_strip[...] = packed([total[n * 8 : n * 8 + 8, :] for n in range(PLANES)])
     strip_copies = send_around(False, *near)
+    row_copies = send_around(True, *near)
     plane_copies = row_copies + strip_copies
 
     for copy in quench_copies:

time: 29.3 us -> 28.7 us (0.980)
  Pallas kernels: 28.6 us -> 28 us
    pallas_call x1, Pallas kernels: 25.7 us -> 25.1 us  [halo_field(): pl.pallas_call(image_kernel, out_shape=jax.ShapeDtypeStruct((2, 3 * ROWS,...]
where the time goes in v4:
time: 28.7 us; the launch traced here: 28.6 us
  Pallas kernels  28 us (98%)
  between operations  0.64 us (2%)
    pallas_call x1, Pallas kernels, halo_field(): pl.pallas_call(image_kernel, out_shape=jax.ShapeDtypeStruct((2, 3 * ROWS,...  25.1 us
    pallas_call x1, Pallas kernels, baked(): pl.pallas_call(bake_kernel, out_shape=(out, out, out), in_specs=[pl.Block...  2.89 us

profile of v4, /device:TPU:1, one launch (start us, length us, event | category | flops | bytes accessed | tf_op | source)
XLA Modules:
  0.0 28.6 jit_solution(6055293943879998428)
XLA Ops:
  0.6 25.1 %image.1.start = f32[2,24,16,256]{3,2,1,0:T(8,128)S(1)} custom-call(s32[2,4]{1,0:T(2,128)} %bitcast.2, s32[2,4]{1,0:T(2,128)} %bitcast.3, f32[32]{0:T(128)} %weight_hbm.1, f32[2,4]{1,0:T(2,128)} %levels_hbm.1, s32[128,128]{1,0:T(8,128)} %codes_hbm.1, bf16[2,2,128,128]{3,2,1,0:T(8,128)(2,1)} %constant.12.clone.cell_waves_hbm, ...), custom_call_target="tpu_custom_call" | custom-call | tf_op jit(solution)/shard_map/image/pallas_call | solution.py:536
  25.7 2.9 %bake.1 = (f32[8,16,128]{2,1,0:T(8,128)}, f32[8,16,128]{2,1,0:T(8,128)}, f32[8,16,128]{2,1,0:T(8,128)}) custom-call(f32[2,24,16,256]{3,2,1,0:T(8,128)S(1)} %image.1.start), custom_call_target="tpu_custom_call" | custom-call | tf_op jit(solution)/shard_map/bake/pallas_call | solution.py:683

commit v5 on v4

--- a/solution.py
+++ b/solution.py
@@ -333,15 +333,16 @@
             half_ref[span, :], right_ref[...], preferred_element_type=jnp.float32
         )
 
-    def gather(j, wave, p):
+    def gather(j, wave, p, parts=(0, 1, 2)):
         at = p * ROWS
-        if j == count - 1:
+        final = j == count - 1 and parts[-1] == 2
+        if final:
             at = pl.multiple_of(at, ROWS)
         weight = weight_ref[src * count + j] * norm
         real = ((0, 0), (1, 1), (0, 2), (2, 2), (0, 4), (1, 3), (3, 3), (2, 4), (4, 4))
         imag = ((1, 0), (1, 2), (3, 0), (1, 4), (3, 2), (3, 4))
         total = {}
-        for c in range(3):
+        for c in parts:
             re, im = [], []
             for n in range(TERMS):
                 rows = pl.ds((c * TERMS + n) * 64 + at, ROWS)
@@ -349,10 +350,10 @@
                 im.append(wave[rows, COLS : 2 * COLS])
             for a, b in real:
                 value = re[a] * re[b] + im[a] * im[b]
-                total[a, b] = value if c == 0 else total[a, b] + value
+                total[a, b] = value if c == parts[0] else total[a, b] + value
             for a, b in imag:
                 value = im[a] * re[b] - re[a] * im[b]
-                total[-a - 1, b] = value if c == 0 else total[-a - 1, b] + value
+                total[-a - 1, b] = value if c == parts[0] else total[-a - 1, b] + value
 
         def part(a, b, factor):
             sign = a if a >= 0 else -a - 1
@@ -373,7 +374,7 @@
             planes = [
                 planes[n] + acc_ref[p, n * ROWS : (n + 1) * ROWS, :] for n in range(PLANES)
             ]
-        if j < count - 1:
+        if not final:
             for n in range(PLANES):
                 acc_ref[p, n * ROWS : (n + 1) * ROWS, :] = planes[n]
         else:
@@ -435,6 +436,9 @@
                 gather(j - 1, waves[(j - 1) % 2], step // 2)
             if step in (5, 10, 15):
                 second(waves[j % 2], step // 5 - 1)
+            if j == count - 1 and step > 10:
+                for p in range(8 * (step - 11) // 5, 8 * (step - 10) // 5):
+                    gather(j, waves[j % 2], p, (0, 1))
         if j == EARLY:
             pl.semaphore_wait(barrier, len(peers) + len(around))
             loads["quench"].wait()
@@ -458,7 +462,7 @@
     exchange = []
     for d in (4, 5, 3, 6, 2, 7, 1, 0):
         peer = lax.rem(src + d, N_SRC)
-        gather(count - 1, waves[(count - 1) % 2], peer)
+        gather(count - 1, waves[(count - 1) % 2], peer, (2,))
         if d > 0:
             copy = pltpu.make_async_remote_copy(
                 src_ref=planes_ref.at[peer],
@@ -511,13 +515,14 @@
             field[0, g * 8 + r, :, side * COLS : (side + 1) * COLS] = acid
 
     start_acid(1, lambda n: own_planes[n * 8 : n * 8 + 8, :], 0)
-    for copy in row_copies:
-        copy.wait_recv()
     for g in (0, 2):
+        row_copies[0 if g == 2 else 1].wait_recv()
         start_acid(g, lambda n: near_planes[g // 2, n * 8 : n * 8 + 8, :], 0)
-    for copy in strip_copies:
-        copy.wait_recv()
-    for g in range(3):
+    corners = [shift for shift in AROUND if shift[1] != 0]
+    for g in (1, 0, 2):
+        for (dr, _), copy in zip(corners, strip_copies):
+            if 1 - dr == g:
+                copy.wait_recv()
         merged = jnp.where(first_half, near_strips[2 * g], near_strips[2 * g + 1])
         tiles = [unpacked(merged, n) for n in range(PLANES)]
         start_acid(g, lambda n: tiles[n], 1)

time: 28.7 us -> 28.6 us (level)
  no operation moved by 1% of the time
where the time goes in v5:
time: 28.6 us; the launch traced here: 28.5 us
  Pallas kernels  27.9 us (98%)
  between operations  0.64 us (2%)
    pallas_call x1, Pallas kernels, halo_field(): pl.pallas_call(image_kernel, out_shape=jax.ShapeDtypeStruct((2, 3 * ROWS,...  25 us
    pallas_call x1, Pallas kernels, baked(): pl.pallas_call(bake_kernel, out_shape=(out, out, out), in_specs=[pl.Block...  2.89 us

profile of v5, /device:TPU:1, one launch (start us, length us, event | category | flops | bytes accessed | tf_op | source)
XLA Modules:
  0.0 28.5 jit_solution(8776376018008885285)
XLA Ops:
  0.6 25.0 %image.1.start = f32[2,24,16,256]{3,2,1,0:T(8,128)S(1)} custom-call(s32[2,4]{1,0:T(2,128)} %bitcast.2, s32[2,4]{1,0:T(2,128)} %bitcast.3, f32[32]{0:T(128)} %weight_hbm.1, f32[2,4]{1,0:T(2,128)} %levels_hbm.1, s32[128,128]{1,0:T(8,128)} %codes_hbm.1, bf16[2,2,128,128]{3,2,1,0:T(8,128)(2,1)} %constant.12.clone.cell_waves_hbm, ...), custom_call_target="tpu_custom_call" | custom-call | tf_op jit(solution)/shard_map/image/pallas_call | solution.py:541
  25.6 2.9 %bake.1 = (f32[8,16,128]{2,1,0:T(8,128)}, f32[8,16,128]{2,1,0:T(8,128)}, f32[8,16,128]{2,1,0:T(8,128)}) custom-call(f32[2,24,16,256]{3,2,1,0:T(8,128)S(1)} %image.1.start), custom_call_target="tpu_custom_call" | custom-call | tf_op jit(solution)/shard_map/bake/pallas_call | solution.py:688
